TPU v7x, 128 devices: a whole 4x4x4 slice. The times are simulated.
128 devices in a mesh: row: 16 (over y, x), col: 8 (over z, core).
Axes of the slice: x: 4, y: 4, z: 4, core: 2. Of those that a mesh axis runs over, the one named last changes fastest.
Arguments:
- phase: float32 [8192, 4096], P('row', 'col'), may hold values from -1 to 1
- tile_mask: int32 [32, 16], P('row', 'col'), may hold values 0 or 1
Outputs:
- updated: float32 [8192, 4096], P('row', 'col')
- section: float32 [8192, 4096], P('row', 'col')
All inputs are finite; a program needn't handle non-finite values. No bound on the sum of `tile_mask` on one device may be relied on, other than what follows from the above.
Results may differ from a plain program's by a relative error of at most 0.0003.
Values sent between devices are 32-bit elements; how exact they have to be, the bound alone decides.
No kernel may reach another device: no remote copies, remote signals or barrier semaphores. Data moves between devices by JAX's collectives and lax.ppermute only.
A program may use at most 64 MiB of HBM per device.

v0:
```python
import functools

import jax
import jax.numpy as jnp
from jax import lax
from jax.experimental import pallas as pl
from jax.experimental.pallas import tpu as pltpu
from jax.sharding import Mesh
from jax.sharding import PartitionSpec as P

TILE = 256
ROW = ("row_0", "row_1")
COL = ("col_0", "col_1")
ALL = ROW + COL
HALO = 8
LANES = 128
UNROLL = 4


def splat(row, lane, k):
    return jnp.broadcast_to(
        jnp.sum(jnp.where(lane == k, row, 0.0), axis=1, keepdims=True), (8, LANES)
    )


def matmul3(a, b):
    return [
        [a[i][0] * b[0][j] + a[i][1] * b[1][j] + a[i][2] * b[2][j] for j in range(3)]
        for i in range(3)
    ]


def phi_column(hess, scale, order):
    inv = 1.0 / 1024.0
    base = [[hess[i][j] * (scale * inv) for j in range(3)] for i in range(3)]
    zero = jnp.zeros((8, LANES), jnp.float32)
    term = base
    cols = [[zero + inv, zero, zero]] + [[zero] * 3 for _ in range(order - 1)]
    total = base
    sums = cols
    for degree in range(2, 11):
        first = [term[i][0] * (inv / degree) for i in range(3)]
        cols = [first] + [[c * (inv / degree) for c in col] for col in cols[:-1]]
        term = [[v * (1.0 / degree) for v in row] for row in matmul3(term, base)]
        total = [[total[i][j] + term[i][j] for j in range(3)] for i in range(3)]
        sums = [[s + c for s, c in zip(sc, cc)] for sc, cc in zip(sums, cols)]
    one, two = inv, 0.5 * inv * inv
    for _ in range(10):
        moved = []
        for n, col in enumerate(sums):
            new = [
                2.0 * col[i]
                + (total[i][0] * col[0] + total[i][1] * col[1] + total[i][2] * col[2])
                for i in range(3)
            ]
            if n >= 1:
                new = [new[i] + sums[n - 1][i] * one for i in range(3)]
            if n >= 2:
                new = [new[i] + sums[n - 2][i] * two for i in range(3)]
            moved.append(new)
        square = matmul3(total, total)
        total = [[2.0 * total[i][j] + square[i][j] for j in range(3)] for i in range(3)]
        sums = moved
        one, two = 2.0 * one, 2.0 * two + one * one
    return sums[-1]


def hessenberg(gathered):
    lane = lax.broadcasted_iota(jnp.int32, (8, LANES), 1)
    row = jnp.broadcast_to(jnp.sum(gathered, axis=0, keepdims=True), (8, LANES))
    g = {}
    for n, (i, j) in enumerate(PAIRS):
        g[i, j] = splat(row, lane, n)
    r = {}
    r[0, 0] = jnp.sqrt(g[0, 0])
    for m in (1, 2, 3):
        r[0, m] = g[0, m] / r[0, 0]
    r[1, 1] = jnp.sqrt(jnp.maximum(g[1, 1] - r[0, 1] * r[0, 1], 1e-9 * g[1, 1]))
    for m in (2, 3):
        r[1, m] = (g[1, m] - r[0, 1] * r[0, m]) / r[1, 1]
    r[2, 2] = jnp.sqrt(
        jnp.maximum(g[2, 2] - r[0, 2] * r[0, 2] - r[1, 2] * r[1, 2], 1e-9 * g[2, 2])
    )
    r[2, 3] = (g[2, 3] - r[0, 2] * r[0, 3] - r[1, 2] * r[1, 3]) / r[2, 2]
    zero = jnp.zeros((8, LANES), jnp.float32)
    c0 = [8.0 * r[0, 1] / r[0, 0], 8.0 * r[1, 1] / r[0, 0], zero]
    c1 = [(8.0 * r[0, 2] - c0[0] * r[0, 1]) / r[1, 1], (8.0 * r[1, 2] - c0[1] * r[0, 1]) / r[1, 1], 8.0 * r[2, 2] / r[1, 1]]
    c2 = [
        (8.0 * r[0, 3] - c0[0] * r[0, 2] - c1[0] * r[1, 2]) / r[2, 2],
        (8.0 * r[1, 3] - c0[1] * r[0, 2] - c1[1] * r[1, 2]) / r[2, 2],
        (8.0 * r[2, 3] - c1[2] * r[1, 2]) / r[2, 2],
    ]
    hess = [[c0[i], c1[i], c2[i]] for i in range(3)]
    for i in range(3):
        hess[i][i] = hess[i][i] - 8.0
    return r, hess


PAIRS = tuple((i, j) for i in range(3) for j in range(i, 4))


def on_basis(r, weights, factor):
    scale = factor * r[0, 0]
    d2 = weights[2] / r[2, 2]
    d1 = (weights[1] - r[1, 2] * d2) / r[1, 1]
    d0 = (weights[0] - r[0, 1] * d1 - r[0, 2] * d2) / r[0, 0]
    return [d0 * scale, d1 * scale, d2 * scale]


def around(ref, at):
    tiles = ref.shape[0]
    lane = lax.broadcasted_iota(jnp.int32, (8, LANES), 1)
    mids = [ref[j, pl.ds(at, 8), :] for j in range(tiles)]
    ones = [pltpu.roll(m, 1, 1) for m in mids]
    backs = [pltpu.roll(m, LANES - 1, 1) for m in mids]
    out = []
    for j in range(tiles):
        left = jnp.where(lane == 0, ones[j - 1], ones[j])
        right = jnp.where(lane == LANES - 1, backs[(j + 1) % tiles], backs[j])
        rows = ref[j, pl.ds(at - 1, 8), :] + ref[j, pl.ds(at + 1, 8), :]
        out.append((left + right) + rows)
    return mids, out


def write_sums(sums, out_ref):
    lane = lax.broadcasted_iota(jnp.int32, (1, LANES), 1)
    row = jnp.zeros((1, LANES), jnp.float32)
    for n, s in enumerate(sums):
        row = row + jnp.where(lane == n, jnp.sum(s), 0.0)
    out_ref[...] = jnp.broadcast_to(row, out_ref.shape)


def for_bands(n, body, init=0, halo=True):
    count = n // TILE
    carry = init
    if halo:
        carry = body(8, 0, carry)
    for t in range(count):

        def group(i, c, t=t):
            at = 16 + t * TILE + i * (8 * UNROLL)
            for u in range(UNROLL):
                c = body(at + 8 * u, t + 1, c)
            return c

        carry = lax.fori_loop(0, TILE // (8 * UNROLL), group, carry)
    if halo:
        carry = body(n + 16, count + 1, carry)
    return carry


def act_of(act_ref, band):
    return [act_ref[j, band : band + 1, :] for j in range(act_ref.shape[0])]


def powers_and_sums(fields, coef_ref, act_ref, n):
    w0, w1, w2 = fields
    tiles = w0.shape[0]

    def apply(src, dst):
        def body(at, band, c):
            mids, sides = around(src, at)
            for j, act in enumerate(act_of(act_ref, band)):
                dst[j, pl.ds(at, 8), :] = (0.25 * act) * sides[j] + coef_ref[j, pl.ds(at, 8), :] * mids[j]
            return c

        return body

    for_bands(n, apply(w0, w1))
    for_bands(n, apply(w1, w2))

    def last(at, band, sums):
        mids, sides = around(w2, at)
        acts = act_of(act_ref, band)
        sums = list(sums)
        for j in range(tiles - 1):
            here = pl.ds(at, 8)
            third = (0.25 * acts[j]) * sides[j] + coef_ref[j, here, :] * mids[j]
            basis = [w0[j, here, :], w1[j, here, :], mids[j], third]
            for k, (a, b) in enumerate(PAIRS):
                sums[k] = sums[k] + basis[a] * basis[b]
        return tuple(sums)

    zero = jnp.zeros((8, LANES), jnp.float32)
    return for_bands(n, last, tuple(zero for _ in PAIRS), halo=False)


def strips_kernel(left_ref, right_ref, mask_ref, to_left_ref, to_right_ref):
    n = left_ref.shape[0]
    lane = lax.broadcasted_iota(jnp.int32, (8, LANES), 1)
    for ref, out, rows, col in ((left_ref, to_left_ref, 0, 0), (right_ref, to_right_ref, 120, mask_ref.shape[1] - 1)):
        out[:, :n] = ref[...].T[rows : rows + 8, :]
        extra = jnp.zeros((8, LANES), jnp.float32)
        for t in range(mask_ref.shape[0]):
            extra = extra + jnp.where(lane == t, mask_ref[t, col].astype(jnp.float32), 0.0)
        out[:, n:] = extra


def corners_kernel(from_left_ref, from_right_ref, top_ref, bottom_ref, mask_ref, side_ref, up_ref, down_ref):
    n = side_ref.shape[0]
    width = top_ref.shape[1]
    tiles_r, tiles_c = mask_ref.shape
    zeros = jnp.zeros((LANES - 16, n), jnp.float32)
    side = jnp.concatenate([from_right_ref[:, :n], zeros, from_left_ref[:, :n]], axis=0).T
    side_ref[...] = side
    lane = lax.broadcasted_iota(jnp.int32, (8, LANES), 1)
    from_left = from_left_ref[:, n:]
    from_right = from_right_ref[:, n:]
    for ref, out, rows, t in ((top_ref, up_ref, 0, 0), (bottom_ref, down_ref, n - 8, tiles_r - 1)):
        out[:, :width] = ref[...]
        extra = side[rows : rows + 8, :]
        for c in range(tiles_c):
            extra = jnp.where(lane == 16 + c, mask_ref[t, c].astype(jnp.float32), extra)
        extra = jnp.where(lane == 16 + tiles_c, splat(from_right, lane, t), extra)
        extra = jnp.where(lane == 17 + tiles_c, splat(from_left, lane, t), extra)
        out[:, width:] = extra


def first_kernel(
    phase_ref, side_ref, up_ref, down_ref, from_left_ref, from_right_ref, mask_ref,
    p_ref, w0, w1, w2, coef_ref, act_ref, sums_ref,
):
    n, width = phase_ref.shape
    tiles = p_ref.shape[0]
    tiles_r, tiles_c = mask_ref.shape
    lane = lax.broadcasted_iota(jnp.int32, (8, LANES), 1)

    def cells(band, values, right, left):
        for j in range(tiles - 1):
            act_ref[j, band : band + 1, :] = jnp.full((1, LANES), values[j * LANES // TILE])
        ends = jnp.where(lane < 8, right, jnp.where(lane >= LANES - 8, left, 0.0))
        act_ref[tiles - 1, band : band + 1, :] = ends[0:1]

    def pick(ref, at, k):
        return jnp.sum(jnp.where(lane == k, ref[:, at:], 0.0)[0:1, :])

    for t, ref in ((0, up_ref), (tiles_r + 1, down_ref)):
        values = [pick(ref, width, 16 + c) for c in range(tiles_c + 2)]
        cells(t, values[:tiles_c], values[tiles_c], values[tiles_c + 1])
    for t in range(tiles_r):
        values = [mask_ref[t, c].astype(jnp.float32) for c in range(tiles_c)]
        cells(t + 1, values, pick(from_right_ref, n, t), pick(from_left_ref, n, t))

    blank = jnp.zeros((8, LANES), jnp.float32)
    for ref in (p_ref, w0, w1, w2):
        for j in range(tiles):
            ref[j, 0:8, :] = blank
            ref[j, n + 24 : n + 32, :] = blank
    for at, ref in ((8, up_ref), (n + 16, down_ref)):
        for j in range(tiles - 1):
            p_ref[j, at : at + 8, :] = ref[:, j * LANES : (j + 1) * LANES]
        p_ref[tiles - 1, at : at + 8, :] = jnp.where((lane < 8) | (lane >= LANES - 8), ref[:, width:], 0.0)
    for j in range(tiles - 1):
        p_ref[j, 16 : n + 16, :] = phase_ref[:, j * LANES : (j + 1) * LANES]
    p_ref[tiles - 1, 16 : n + 16, :] = side_ref[...]

    def force(at, band, c):
        mids, sides = around(p_ref, at)
        for j, act in enumerate(act_of(act_ref, band)):
            square = mids[j] * mids[j]
            w0[j, pl.ds(at, 8), :] = act * (2.0 * sides[j] - (7.0 + square) * mids[j])
            coef_ref[j, pl.ds(at, 8), :] = act * (0.125 - 0.375 * square)
        return c

    for_bands(n, force)
    write_sums(powers_and_sums((w0, w1, w2), coef_ref, act_ref, n), sums_ref)


def second_kernel(
    gathered_ref, p_ref, w0, w1, w2, coef_ref, act_ref,
    section_ref, base_ref, v0, v1, v2, sums_ref,
):
    n, width = section_ref.shape
    tiles = p_ref.shape[0]
    r, hess = hessenberg(gathered_ref[...])
    lane = lax.broadcasted_iota(jnp.int32, (8, LANES), 1)
    half = lane < LANES // 2
    scale = jnp.where(half, 0.5, 1.0)
    weights = phi_column(hess, scale, 1)
    coefs = on_basis(r, weights, scale)
    a = [jnp.max(jnp.where(half, c, -jnp.inf)) for c in coefs]
    f = [jnp.max(jnp.where(half, -jnp.inf, c)) for c in coefs]
    blank = jnp.zeros((8, LANES), jnp.float32)
    for ref in (v0, v1, v2):
        for j in range(tiles):
            ref[j, 0:8, :] = blank
            ref[j, n + 24 : n + 32, :] = blank

    def start(at, band, c):
        acts = act_of(act_ref, band)
        here = pl.ds(at, 8)
        for j in range(tiles):
            ws = [ref[j, here, :] for ref in (w0, w1, w2)]
            phase = p_ref[j, here, :]
            shift = a[0] * ws[0] + a[1] * ws[1] + a[2] * ws[2]
            v0[j, here, :] = -acts[j] * (shift * shift) * (shift + 3.0 * phase)
            if j < tiles - 1 and 1 <= band <= n // TILE:
                to = pl.ds(pl.multiple_of(at - 16, 8), 8)
                cols = slice(j * LANES, (j + 1) * LANES)
                first = f[0] * ws[0] + f[1] * ws[1] + f[2] * ws[2]
                section_ref[to, cols] = phase + shift
                base_ref[to, cols] = phase + first
        return c

    for_bands(n, start)
    write_sums(powers_and_sums((v0, v1, v2), coef_ref, act_ref, n), sums_ref)


def third_kernel(gathered_ref, base_ref, v0, v1, v2, updated_ref):
    n, width = base_ref.shape
    r, hess = hessenberg(gathered_ref[...])
    coefs = on_basis(r, phi_column(hess, 1.0, 3), 32.0)
    d = [jnp.max(c) for c in coefs]

    def body(at, band, c):
        to = pl.ds(pl.multiple_of(at - 16, 8), 8)
        for j in range(width // LANES):
            vs = [ref[j, pl.ds(at, 8), :] for ref in (v0, v1, v2)]
            cols = slice(j * LANES, (j + 1) * LANES)
            updated_ref[to, cols] = base_ref[to, cols] + (d[0] * vs[0] + d[1] * vs[1] + d[2] * vs[2])
        return c

    for_bands(n, body, halo=False)


def params(mib):
    return pltpu.CompilerParams(vmem_limit_bytes=mib << 20)


VM = pl.BlockSpec(memory_space=pltpu.VMEM)
SM = pl.BlockSpec(memory_space=pltpu.SMEM)


def both_ways(low, high, axis):
    size = lax.axis_size(axis)
    up = [(i, i + 1) for i in range(size - 1)]
    return lax.ppermute(high, axis, up), lax.ppermute(low, axis, [(b, a) for a, b in up])


def total(sums):
    size = sums.shape[0]
    sent = lax.all_to_all(sums.reshape(size, 1, LANES), ALL, 0, 0, tiled=True)
    return sent.reshape(size, LANES)


def body(phase, tile_mask):
    n, width = phase.shape
    f32 = jnp.float32
    sd = jax.ShapeDtypeStruct
    to_left, to_right = pl.pallas_call(
        strips_kernel,
        grid=(1,),
        in_specs=[
            pl.BlockSpec((n, LANES), lambda i: (0, 0)),
            pl.BlockSpec((n, LANES), lambda i: (0, width // LANES - 1)),
            SM,
        ],
        out_shape=[sd((8, n + LANES), f32)] * 2,
        compiler_params=params(4),
        name="strips",
    )(phase, phase, tile_mask)
    from_left, from_right = both_ways(to_left, to_right, COL)
    side, to_up, to_down = pl.pallas_call(
        corners_kernel,
        in_specs=[VM] * 4 + [SM],
        out_shape=[sd((n, LANES), f32)] + [sd((8, width + LANES), f32)] * 2,
        compiler_params=params(4),
        name="corners",
    )(from_left, from_right, phase[:8], phase[n - 8 :], tile_mask)
    from_up, from_down = both_ways(to_up, to_down, ROW)
    devices = 1
    for axis in ALL:
        devices *= lax.axis_size(axis)
    tiles = width // LANES + 1
    ext = sd((tiles, n + 32, LANES), f32)
    act = sd((tiles, 8, LANES), f32)
    sums = sd((devices, LANES), f32)
    p, w0, w1, w2, coef, act, part = pl.pallas_call(
        first_kernel,
        in_specs=[VM] * 6 + [SM],
        out_specs=[VM] * 7,
        out_shape=[ext, ext, ext, ext, ext, act, sums],
        compiler_params=params(20),
        name="first",
    )(phase, side, from_up, from_down, from_left, from_right, tile_mask)
    own = sd((n, width), f32)
    section, base, v0, v1, v2, part = pl.pallas_call(
        second_kernel,
        in_specs=[VM] * 7,
        out_specs=[VM] * 6,
        out_shape=[own, own, ext, ext, ext, sums],
        compiler_params=params(24),
        name="second",
    )(total(part), p, w0, w1, w2, coef, act)
    updated = pl.pallas_call(
        third_kernel,
        in_specs=[VM] * 5,
        out_specs=VM,
        out_shape=own,
        compiler_params=params(12),
        name="third",
    )(total(part), base, v0, v1, v2)
    return updated, section


def solution(mesh):
    split = Mesh(mesh.devices.reshape(4, 4, 4, 2), ALL)
    in_specs = (P(ROW, COL), P(ROW, COL))
    out_specs = (P(ROW, COL), P(ROW, COL))
    return jax.shard_map(body, mesh=split, in_specs=in_specs, out_specs=out_specs, check_vma=False)
```

profile of v0, /device:TPU:1, one launch (start us, length us, event | category | flops | bytes accessed | tf_op | source)
XLA Modules:
  0.0 74.5 jit_solution(4593180744109716414)
XLA Ops:
  0.6 0.0 copy-start
  0.6 1.2 %copy-done = f32[512,512]{1,0:T(8,128)S(1)} copy-done((f32[512,512]{1,0:T(8,128)S(1)}, f32[512,512]{1,0:T(8,128)}, u32[]{:S(2)}) %copy-start) | copy-done | bytes 1048600
  1.9 0.0 copy-start.2
  1.9 0.7 copy-done.2
  2.5 0.0 copy-start.1
  2.5 0.0 copy-start.3
  2.5 0.7 strips.1
  3.3 4.9 %collective-permute-start = (f32[8,640]{1,0:T(8,128)S(1)}, f32[8,640]{1,0:T(8,128)S(1)}, u32[]{:S(2)}, u32[]{:S(2)}) collective-permute-start(f32[8,640]{1,0:T(8,128)S(1)} %get-tuple-element.20), channel_id=1, source_target_pairs={{0,1},{1,2},{2,3},{3,4},{4,5},{5,6},{6,7},{8,9},{9,10},{10,11},{11... | collective-permute-start | bytes 61448 | tf_op jit(solution)/shard_map/ppermute | solution.py:337
  8.2 1.9 %collective-permute-start.1 = (f32[8,640]{1,0:T(8,128)S(1)}, f32[8,640]{1,0:T(8,128)S(1)}, u32[]{:S(2)}, u32[]{:S(2)}) collective-permute-start(f32[8,640]{1,0:T(8,128)S(1)} %get-tuple-element.21), channel_id=1, source_target_pairs={{1,0},{2,1},{3,2},{4,3},{5,4},{6,5},{7,6},{9,8},{10,9},{11,10},{12... | collective-permute-start | bytes 61448 | tf_op jit(solution)/shard_map/ppermute | solution.py:337
  10.1 0.0 copy-done.1
  10.2 0.0 collective-permute-done.from_left_ref
  10.2 3.1 %collective-permute-done.1.from_right_ref = f32[8,640]{1,0:T(8,128)S(1)} collective-permute-done((f32[8,640]{1,0:T(8,128)S(1)}, f32[8,640]{1,0:T(8,128)S(1)}, u32[]{:S(2)}, u32[]{:S(2)}) %collective-permute-start.1) | collective-permute-done | bytes 20512 | tf_op jit(solution)/shard_map/ppermute | solution.py:337
  13.3 0.0 copy-done.3
  13.3 0.7 corners.1
  14.0 3.1 %collective-permute-start.2 = (f32[8,640]{1,0:T(8,128)S(1)}, f32[8,640]{1,0:T(8,128)S(1)}, u32[]{:S(2)}, u32[]{:S(2)}) collective-permute-start(f32[8,640]{1,0:T(8,128)S(1)} %get-tuple-element.23), channel_id=1, source_target_pairs={{0,8},{8,16},{16,24},{24,32},{32,40},{40,48},{48,56},{56,64},{64,7... | collective-permute-start | bytes 61448 | tf_op jit(solution)/shard_map/ppermute | solution.py:337
  17.2 1.3 %collective-permute-start.3 = (f32[8,640]{1,0:T(8,128)S(1)}, f32[8,640]{1,0:T(8,128)S(1)}, u32[]{:S(2)}, u32[]{:S(2)}) collective-permute-start(f32[8,640]{1,0:T(8,128)S(1)} %get-tuple-element.24), channel_id=1, source_target_pairs={{8,0},{16,8},{24,16},{32,24},{40,32},{48,40},{56,48},{64,56},{72,6... | collective-permute-start | bytes 61448 | tf_op jit(solution)/shard_map/ppermute | solution.py:337
  18.5 0.0 collective-permute-done.2.up_ref
  18.5 3.2 %collective-permute-done.3.down_ref = f32[8,640]{1,0:T(8,128)S(1)} collective-permute-done((f32[8,640]{1,0:T(8,128)S(1)}, f32[8,640]{1,0:T(8,128)S(1)}, u32[]{:S(2)}, u32[]{:S(2)}) %collective-permute-start.3) | collective-permute-done | bytes 20512 | tf_op jit(solution)/shard_map/ppermute | solution.py:337
  21.7 8.5 %first.1 = (f32[5,544,128]{2,1,0:T(8,128)S(1)}, f32[5,544,128]{2,1,0:T(8,128)S(1)}, f32[5,544,128]{2,1,0:T(8,128)S(1)}, f32[5,544,128]{2,1,0:T(8,128)S(1)}, f32[...) custom-call(f32[512,512]{1,0:T(8,128)S(1)} %copy-done.1, ...), custom_call_target="tpu_custom_call" | custom-call | tf_op jit(solution)/shard_map/first/pallas_call | solution.py:378
  30.2 20.7 %all_to_all.10 = f32[128,1,128]{2,1,0:T(1,128)S(1)} all-to-all(f32[128,1,128]{2,1,0:T(1,128)S(1)} %bitcast.11), channel_id=1, replica_groups=mesh['row_0'=4,'row_1'=4,'col_0'=4,'col_1'=2] {'row_0','row_1','col_0','..., dimensions={0} | all-to-all | bytes 131072 | tf_op jit(solution)/shard_map/all_to_all | solution.py:342
  50.9 8.0 %second.1 = (f32[512,512]{1,0:T(8,128)}, f32[512,512]{1,0:T(8,128)S(1)}, f32[5,544,128]{2,1,0:T(8,128)S(1)}, f32[5,544,128]{2,1,0:T(8,128)S(1)}, f32[5,544,128]{2,1,0:T(8,128)S(1)}, /*index=5*/f32[128,128]{1,0:T(8,128)S(1)}) custom-call(f32[128,128]{1,0:T(8,128)S(1)} %bitcast.8, f32[5,544,128]{2,1,0:T(8,128)S(1)} %get-tuple-element.26.p_ref, ...), custom_call_target="tpu_custom_call" | custom-call | tf_op jit(solution)/shard_map/second/pallas_call | solution.py:387
  58.9 13.8 %all_to_all.11 = f32[128,1,128]{2,1,0:T(1,128)S(1)} all-to-all(f32[128,1,128]{2,1,0:T(1,128)S(1)} %bitcast.10), channel_id=1, replica_groups=mesh['row_0'=4,'row_1'=4,'col_0'=4,'col_1'=2] {'row_0','row_1','col_0','..., dimensions={0} | all-to-all | bytes 131072 | tf_op jit(solution)/shard_map/all_to_all | solution.py:342
  72.8 1.8 %third.1 = f32[512,512]{1,0:T(8,128)} custom-call(f32[128,128]{1,0:T(8,128)S(1)} %bitcast.9, f32[512,512]{1,0:T(8,128)S(1)} %get-tuple-element.33.base_ref, f32[5,544,128]{2,1,0:T(8,128)S(1)} %get-tuple-element.34.v0, f32[5,544,128]{2,1,0:T(8,128)S(1)} %get-tuple-element.35.v1, f32[5,544,128]{2,1,0:T(8,128)S(1)} %get-tuple-element.36.v2), custom_call_target="tpu_custom_call" | custom-call | tf_op jit(solution)/shard_map/third/pallas_call | solution.py:395
  (1 shorter events, 0.0 us)
Async XLA Ops:
  0.6 1.2 %copy-start = (f32[512,512]{1,0:T(8,128)S(1)}, f32[512,512]{1,0:T(8,128)}, u32[]{:S(2)}) copy-start(f32[512,512]{1,0:T(8,128)} %phase_ref.1) | copy-start | bytes 3145732
  1.9 0.7 copy-start.2
  2.5 7.6 %copy-start.1 = (f32[512,512]{1,0:T(8,128)S(1)}, f32[512,512]{1,0:T(8,128)}, u32[]{:S(2)}) copy-start(f32[512,512]{1,0:T(8,128)} %phase_ref.1) | copy-start | bytes 3145732
  2.5 10.8 %copy-start.3 = (s32[2,2]{1,0:T(2,128)S(1)}, s32[2,2]{1,0:T(2,128)}, u32[]{:S(2)}) copy-start(s32[2,2]{1,0:T(2,128)} %mask_ref.5) | copy-start | bytes 52
  3.3 6.9 %collective-permute-start = (f32[8,640]{1,0:T(8,128)S(1)}, f32[8,640]{1,0:T(8,128)S(1)}, u32[]{:S(2)}, u32[]{:S(2)}) collective-permute-start(f32[8,640]{1,0:T(8,128)S(1)} %get-tuple-element.20), channel_id=1, source_target_pairs={{0,1},{1,2},{2,3},{3,4},{4,5},{5,6},{6,7},{8,9},{9,10},{10,11},{11... | collective-permute-start | bytes 61448 | tf_op jit(solution)/shard_map/ppermute | solution.py:337
  8.2 5.1 %collective-permute-start.1 = (f32[8,640]{1,0:T(8,128)S(1)}, f32[8,640]{1,0:T(8,128)S(1)}, u32[]{:S(2)}, u32[]{:S(2)}) collective-permute-start(f32[8,640]{1,0:T(8,128)S(1)} %get-tuple-element.21), channel_id=1, source_target_pairs={{1,0},{2,1},{3,2},{4,3},{5,4},{6,5},{7,6},{9,8},{10,9},{11,10},{12... | collective-permute-start | bytes 61448 | tf_op jit(solution)/shard_map/ppermute | solution.py:337
  14.0 4.4 %collective-permute-start.2 = (f32[8,640]{1,0:T(8,128)S(1)}, f32[8,640]{1,0:T(8,128)S(1)}, u32[]{:S(2)}, u32[]{:S(2)}) collective-permute-start(f32[8,640]{1,0:T(8,128)S(1)} %get-tuple-element.23), channel_id=1, source_target_pairs={{0,8},{8,16},{16,24},{24,32},{32,40},{40,48},{48,56},{56,64},{64,7... | collective-permute-start | bytes 61448 | tf_op jit(solution)/shard_map/ppermute | solution.py:337
  17.2 4.5 %collective-permute-start.3 = (f32[8,640]{1,0:T(8,128)S(1)}, f32[8,640]{1,0:T(8,128)S(1)}, u32[]{:S(2)}, u32[]{:S(2)}) collective-permute-start(f32[8,640]{1,0:T(8,128)S(1)} %get-tuple-element.24), channel_id=1, source_target_pairs={{8,0},{16,8},{24,16},{32,24},{40,32},{48,40},{56,48},{64,56},{72,6... | collective-permute-start | bytes 61448 | tf_op jit(solution)/shard_map/ppermute | solution.py:337
where the time goes:
time: 74.8 us; the launch traced here: 74.5 us
  blocking collectives  34.6 us (46%)
  Pallas kernels  19.7 us (26%)
  starting transfers between devices  11.3 us (15%)
  waiting for transfers between devices  6.36 us (9%)
  local copies, waits for them, and re-layouts  1.91 us (3%)
    all_to_all x2, blocking collectives, total(): sent = lax.all_to_all(sums.reshape(size, 1, LANES), ALL, 0, 0, tiled=True)  34.6 us
    pallas_call x1, Pallas kernels, body(): pl.pallas_call(first_kernel, in_specs=[VM] * 6 + [SM], out_specs=[VM] * 7...  8.53 us
    ppermute x2, starting transfers between devices, both_ways(): lax.ppermute(high, axis, up)  8.05 us
    pallas_call x1, Pallas kernels, body(): pl.pallas_call(second_kernel, in_specs=[VM] * 7, out_specs=[VM] * 6, out_...  8 us
    ppermute x2, waiting for transfers between devices, both_ways(): lax.ppermute(low, axis, [(b, a) for a, b in up])  6.36 us
    ppermute x2, starting transfers between devices, both_ways(): lax.ppermute(low, axis, [(b, a) for a, b in up])  3.21 us
    unnamed x8, local copies, waits for them, and re-layouts  1.9 us
    pallas_call x1, Pallas kernels, body(): pl.pallas_call(third_kernel, in_specs=[VM] * 5, out_specs=VM, out_shape=o...  1.75 us
  transfers between devices with their start and end apart: 4, of which 2 were waited for; matrix products, arithmetic and copies ran while one was open for 0% of the time, Pallas kernels for 0%

commit v1 on v0

v1 whole, which is shorter than its diff:
```python
import functools

import jax
import jax.numpy as jnp
from jax import lax
from jax.experimental import pallas as pl
from jax.experimental.pallas import tpu as pltpu
from jax.sharding import Mesh
from jax.sharding import PartitionSpec as P

TILE = 256
ROW = ("row_0", "row_1")
COL = ("col_0", "col_1")
ALL = ROW + COL
HALO = 8
LANES = 128
UNROLL = 11


def splat(row, lane, k):
    return jnp.broadcast_to(
        jnp.sum(jnp.where(lane == k, row, 0.0), axis=1, keepdims=True), (8, LANES)
    )


def matmul3(a, b):
    return [
        [a[i][0] * b[0][j] + a[i][1] * b[1][j] + a[i][2] * b[2][j] for j in range(3)]
        for i in range(3)
    ]


def phi_column(hess, scale, order):
    inv = 1.0 / 1024.0
    base = [[hess[i][j] * (scale * inv) for j in range(3)] for i in range(3)]
    zero = jnp.zeros((8, LANES), jnp.float32)
    term = base
    cols = [[zero + inv, zero, zero]] + [[zero] * 3 for _ in range(order - 1)]
    total = base
    sums = cols
    for degree in range(2, 11):
        first = [term[i][0] * (inv / degree) for i in range(3)]
        cols = [first] + [[c * (inv / degree) for c in col] for col in cols[:-1]]
        term = [[v * (1.0 / degree) for v in row] for row in matmul3(term, base)]
        total = [[total[i][j] + term[i][j] for j in range(3)] for i in range(3)]
        sums = [[s + c for s, c in zip(sc, cc)] for sc, cc in zip(sums, cols)]
    one, two = inv, 0.5 * inv * inv
    for _ in range(10):
        moved = []
        for n, col in enumerate(sums):
            new = [
                2.0 * col[i]
                + (total[i][0] * col[0] + total[i][1] * col[1] + total[i][2] * col[2])
                for i in range(3)
            ]
            if n >= 1:
                new = [new[i] + sums[n - 1][i] * one for i in range(3)]
            if n >= 2:
                new = [new[i] + sums[n - 2][i] * two for i in range(3)]
            moved.append(new)
        square = matmul3(total, total)
        total = [[2.0 * total[i][j] + square[i][j] for j in range(3)] for i in range(3)]
        sums = moved
        one, two = 2.0 * one, 2.0 * two + one * one
    return sums[-1]


def hessenberg(gathered):
    lane = lax.broadcasted_iota(jnp.int32, (8, LANES), 1)
    row = jnp.broadcast_to(jnp.sum(gathered, axis=0, keepdims=True), (8, LANES))
    moments = [splat(row, lane, n) for n in range(6)]
    g = {(i, j): moments[i + j] for i in range(3) for j in range(i, 4)}
    r = {}
    r[0, 0] = jnp.sqrt(g[0, 0])
    for m in (1, 2, 3):
        r[0, m] = g[0, m] / r[0, 0]
    r[1, 1] = jnp.sqrt(jnp.maximum(g[1, 1] - r[0, 1] * r[0, 1], 1e-9 * g[1, 1]))
    for m in (2, 3):
        r[1, m] = (g[1, m] - r[0, 1] * r[0, m]) / r[1, 1]
    r[2, 2] = jnp.sqrt(
        jnp.maximum(g[2, 2] - r[0, 2] * r[0, 2] - r[1, 2] * r[1, 2], 1e-9 * g[2, 2])
    )
    r[2, 3] = (g[2, 3] - r[0, 2] * r[0, 3] - r[1, 2] * r[1, 3]) / r[2, 2]
    zero = jnp.zeros((8, LANES), jnp.float32)
    c0 = [8.0 * r[0, 1] / r[0, 0], 8.0 * r[1, 1] / r[0, 0], zero]
    c1 = [(8.0 * r[0, 2] - c0[0] * r[0, 1]) / r[1, 1], (8.0 * r[1, 2] - c0[1] * r[0, 1]) / r[1, 1], 8.0 * r[2, 2] / r[1, 1]]
    c2 = [
        (8.0 * r[0, 3] - c0[0] * r[0, 2] - c1[0] * r[1, 2]) / r[2, 2],
        (8.0 * r[1, 3] - c0[1] * r[0, 2] - c1[1] * r[1, 2]) / r[2, 2],
        (8.0 * r[2, 3] - c1[2] * r[1, 2]) / r[2, 2],
    ]
    hess = [[c0[i], c1[i], c2[i]] for i in range(3)]
    for i in range(3):
        hess[i][i] = hess[i][i] - 8.0
    return r, hess


def on_basis(r, weights, factor):
    scale = factor * r[0, 0]
    d2 = weights[2] / r[2, 2]
    d1 = (weights[1] - r[1, 2] * d2) / r[1, 1]
    d0 = (weights[0] - r[0, 1] * d1 - r[0, 2] * d2) / r[0, 0]
    return [d0 * scale, d1 * scale, d2 * scale]


def beside(ref, at, sides):
    tiles = ref.shape[0]
    lane = lax.broadcasted_iota(jnp.int32, (8, LANES), 1)
    mids = [ref[j, pl.ds(at, 8), :] for j in range(tiles)]
    ones = [pltpu.roll(m, 1, 1) for m in mids]
    out = [jnp.where(lane == 0, ones[j - 1], ones[j]) for j in range(tiles)]
    if sides == 2:
        backs = [pltpu.roll(m, LANES - 1, 1) for m in mids]
        out = [o + jnp.where(lane == LANES - 1, backs[(j + 1) % tiles], backs[j]) for j, o in enumerate(out)]
    return out


def write_sums(sums, out_ref):
    lane = lax.broadcasted_iota(jnp.int32, (1, LANES), 1)
    row = jnp.zeros((1, LANES), jnp.float32)
    for n, tiles in enumerate(sums):
        row = row + jnp.where(lane == n, jnp.sum(sum(tiles[1:], tiles[0])), 0.0)
    out_ref[...] = jnp.broadcast_to(row, out_ref.shape)


def band_of(group, bands):
    return jnp.clip((group - 1 + TILE // 8) // (TILE // 8), 0, bands - 1)


def act_of(act_ref, group):
    band = pl.multiple_of(8 * band_of(group, act_ref.shape[1] // 8), 8)
    return [act_ref[j, pl.ds(band, 8), :] for j in range(act_ref.shape[0])]


def stencil_pass(src, side_ref, groups, first, emit, carry, sides=2):
    unroll = UNROLL
    while groups % unroll:
        unroll -= 1
    steps = groups // unroll

    def ahead(group, at):
        for u in range(unroll):
            for j, v in enumerate(beside(src, at + 8 * u, sides)):
                side_ref[j, pl.ds(at + 8 * u, 8), :] = v

    def here(group, at, c):
        for u in range(unroll):
            side = [side_ref[j, pl.ds(at + 8 * u, 8), :] for j in range(src.shape[0])]
            c = emit(group + u, at + 8 * u, side, u, c)
        return c

    def both(i, c):
        group = first + i * unroll
        at = pl.multiple_of(8 + 8 * group, 8)
        c = here(group, at, c)
        ahead(group + unroll, at + 8 * unroll)
        return c

    ahead(first, 8 + 8 * first)
    carry = lax.fori_loop(0, steps - 1, both, carry)
    group = first + (steps - 1) * unroll
    return here(group, 8 + 8 * group, carry)


def add_products(sums, pairs, own):
    out = []
    for row, (a, b) in zip(sums, pairs):
        new = []
        for j, s in enumerate(row):
            product = a[j] * b[j]
            new.append(s + (product if own is None else product * own))
        out.append(tuple(new))
    return tuple(out)


def own_of(group, groups, u, unroll):
    if 0 < u < unroll - 1:
        return None
    return jnp.where((group > 0) & (group < groups - 1), 1.0, 0.0)


def no_sums(count, tiles):
    return tuple(tuple(jnp.zeros((8, LANES), jnp.float32) for _ in range(tiles - 1)) for _ in range(count))


def powers(fields, coef_ref, act_ref, side_ref):
    w0, w1, w2 = fields
    tiles = w0.shape[0]
    groups = (w0.shape[1] - 16) // 8

    def apply(src, dst):
        def emit(group, at, side, u, sums):
            acts = act_of(act_ref, group)
            here = pl.ds(at, 8)
            mids, outs = [], []
            for j in range(tiles):
                mid = src[j, here, :]
                total = side[j] + (src[j, pl.ds(at - 1, 8), :] + src[j, pl.ds(at + 1, 8), :])
                out = acts[j] * total + coef_ref[j, here, :] * mid
                dst[j, here, :] = out
                mids.append(mid)
                outs.append(out)
            own = own_of(group, groups, u, UNROLL)
            return add_products(sums, ((mids, outs), (outs, outs)), own)

        return stencil_pass(src, side_ref, groups, 0, emit, no_sums(2, tiles))

    m1, m2 = apply(w0, w1)
    m3, m4 = apply(w1, w2)

    def emit(group, at, side, u, sums):
        here = pl.ds(at, 8)
        mids, images = [], []
        for j in range(tiles - 1):
            mid = w2[j, here, :]
            images.append(0.5 * (side[j] + w2[j, pl.ds(at - 1, 8), :]) + coef_ref[j, here, :] * mid)
            mids.append(mid)
        return add_products(sums, ((mids, images),), None)

    (m5,) = stencil_pass(w2, side_ref, groups - 2, 1, emit, no_sums(1, tiles), sides=1)
    return [m1, m2, m3, m4, m5]


def strips_kernel(odd_ref, phase_hbm, mask_hbm, near_ref, far_ref, left_ref, right_ref, mask_ref, sems):
    n, width = phase_hbm.shape
    copies = [
        pltpu.make_async_copy(phase_hbm.at[:, 0:LANES], left_ref, sems.at[0]),
        pltpu.make_async_copy(phase_hbm.at[:, width - LANES : width], right_ref, sems.at[1]),
        pltpu.make_async_copy(mask_hbm, mask_ref, sems.at[2]),
    ]
    for c in copies:
        c.start()
    for c in copies:
        c.wait()
    odd = jnp.full((8, LANES), odd_ref[1], jnp.int32) > 0
    odd_n = jnp.full((8, n), odd_ref[1], jnp.int32) > 0
    lane = lax.broadcasted_iota(jnp.int32, (8, LANES), 1)
    strips = []
    for ref, rows, col in ((left_ref, 0, 0), (right_ref, LANES - 8, mask_ref.shape[1] - 1)):
        extra = jnp.zeros((8, LANES), jnp.float32)
        for t in range(mask_ref.shape[0]):
            extra = extra + jnp.where(lane == t, mask_ref[t, col].astype(jnp.float32), 0.0)
        strips.append((ref[...].T[rows : rows + 8, :], extra))
    left, right = strips
    for out, a, b in ((near_ref, left, right), (far_ref, right, left)):
        out[:, :n] = jnp.where(odd_n, a[0], b[0])
        out[:, n:] = jnp.where(odd, a[1], b[1])


def corners_kernel(odd_ref, near_in, far_in, phase_ref, mask_ref, side_ref, near_ref, far_ref, masks_ref):
    n, width = phase_ref.shape
    tiles_r, tiles_c = mask_ref.shape
    odd = jnp.full((8, LANES), odd_ref[1], jnp.int32) > 0
    odd_n = jnp.full((8, n), odd_ref[1], jnp.int32) > 0
    from_left = jnp.where(odd_n, near_in[:, :n], far_in[:, :n])
    from_right = jnp.where(odd_n, far_in[:, :n], near_in[:, :n])
    mask_left = jnp.where(odd, near_in[:, n:], far_in[:, n:])
    mask_right = jnp.where(odd, far_in[:, n:], near_in[:, n:])
    masks_ref[0] = mask_left
    masks_ref[1] = mask_right
    zeros = jnp.zeros((LANES - 16, n), jnp.float32)
    side = jnp.concatenate([from_right, zeros, from_left], axis=0).T
    side_ref[...] = side
    lane = lax.broadcasted_iota(jnp.int32, (8, LANES), 1)
    strips = []
    for rows, t in ((0, 0), (n - 8, tiles_r - 1)):
        extra = side[rows : rows + 8, :]
        for c in range(tiles_c):
            extra = jnp.where(lane == 16 + c, mask_ref[t, c].astype(jnp.float32), extra)
        extra = jnp.where(lane == 16 + tiles_c, splat(mask_right, lane, t), extra)
        extra = jnp.where(lane == 17 + tiles_c, splat(mask_left, lane, t), extra)
        strips.append((phase_ref[rows : rows + 8, :], extra))
    up, down = strips
    odd = jnp.full((8, LANES), odd_ref[0], jnp.int32) > 0
    odd_w = jnp.full((8, width), odd_ref[0], jnp.int32) > 0
    for out, a, b in ((near_ref, up, down), (far_ref, down, up)):
        out[:, :width] = jnp.where(odd_w, a[0], b[0])
        out[:, width:] = jnp.where(odd, a[1], b[1])


def first_kernel(
    odd_ref, phase_ref, side_in, near_in, far_in, masks_ref, mask_ref,
    p_ref, w0, w1, w2, coef_ref, act_ref, sums_ref, side_ref,
):
    n, width = phase_ref.shape
    tiles = p_ref.shape[0]
    groups = n // 8 + 2
    tiles_r, tiles_c = mask_ref.shape
    lane = lax.broadcasted_iota(jnp.int32, (8, LANES), 1)
    odd = jnp.full((8, LANES), odd_ref[0], jnp.int32) > 0
    up = [jnp.where(odd, near_in[:, j * LANES : (j + 1) * LANES], far_in[:, j * LANES : (j + 1) * LANES]) for j in range(tiles)]
    down = [jnp.where(odd, far_in[:, j * LANES : (j + 1) * LANES], near_in[:, j * LANES : (j + 1) * LANES]) for j in range(tiles)]

    def cells(band, values, right, left):
        for j in range(tiles - 1):
            act_ref[j, 8 * band : 8 * band + 8, :] = 0.25 * jnp.broadcast_to(values[j * LANES // TILE], (8, LANES))
        ends = jnp.where(lane < 8, right, jnp.where(lane >= LANES - 8, left, 0.0))
        act_ref[tiles - 1, 8 * band : 8 * band + 8, :] = 0.25 * ends

    for t, extra in ((0, up[-1]), (tiles_r + 1, down[-1])):
        values = [splat(extra, lane, 16 + c) for c in range(tiles_c + 2)]
        cells(t, values[:tiles_c], values[tiles_c], values[tiles_c + 1])
    for t in range(tiles_r):
        values = [mask_ref[t, c].astype(jnp.float32) for c in range(tiles_c)]
        cells(t + 1, values, splat(masks_ref[1], lane, t), splat(masks_ref[0], lane, t))

    blank = jnp.zeros((8, LANES), jnp.float32)
    for ref in (p_ref, w0, w1, w2):
        for j in range(tiles):
            ref[j, 0:8, :] = blank
            ref[j, n + 24 : n + 32, :] = blank
    for at, rows in ((8, up), (n + 16, down)):
        for j in range(tiles - 1):
            p_ref[j, at : at + 8, :] = rows[j]
        p_ref[tiles - 1, at : at + 8, :] = jnp.where((lane < 8) | (lane >= LANES - 8), rows[-1], 0.0)
    for j in range(tiles - 1):
        p_ref[j, 16 : n + 16, :] = phase_ref[:, j * LANES : (j + 1) * LANES]
    p_ref[tiles - 1, 16 : n + 16, :] = side_in[...]

    def force(group, at, side, u, sums):
        acts = act_of(act_ref, group)
        here = pl.ds(at, 8)
        outs = []
        for j in range(tiles):
            mid = p_ref[j, here, :]
            total = side[j] + (p_ref[j, pl.ds(at - 1, 8), :] + p_ref[j, pl.ds(at + 1, 8), :])
            square = mid * mid
            out = acts[j] * (8.0 * total - (28.0 + 4.0 * square) * mid)
            w0[j, here, :] = out
            coef_ref[j, here, :] = acts[j] * (0.5 - 1.5 * square)
            outs.append(out)
        return add_products(sums, ((outs, outs),), own_of(group, groups, u, UNROLL))

    (m0,) = stencil_pass(p_ref, side_ref, groups, 0, force, no_sums(1, tiles))
    write_sums([m0] + powers((w0, w1, w2), coef_ref, act_ref, side_ref), sums_ref)


def second_kernel(
    gathered_ref, p_ref, w0, w1, w2, coef_ref, act_ref,
    section_ref, base_ref, v0, v1, v2, sums_ref, side_ref,
):
    n, width = section_ref.shape
    tiles = p_ref.shape[0]
    r, hess = hessenberg(gathered_ref[...])
    lane = lax.broadcasted_iota(jnp.int32, (8, LANES), 1)
    half = lane < LANES // 2
    scale = jnp.where(half, 0.5, 1.0)
    weights = phi_column(hess, scale, 1)
    coefs = on_basis(r, weights, scale)
    a = [jnp.max(jnp.where(half, c, -jnp.inf)) for c in coefs]
    f = [jnp.max(jnp.where(half, -jnp.inf, c)) for c in coefs]
    blank = jnp.zeros((8, LANES), jnp.float32)
    for ref in (v0, v1, v2):
        for j in range(tiles):
            ref[j, 0:8, :] = blank
            ref[j, n + 24 : n + 32, :] = blank

    def start(group, own, sums):
        at = pl.multiple_of(8 + 8 * group, 8)
        acts = act_of(act_ref, group)
        here = pl.ds(at, 8)
        outs = []
        for j in range(tiles):
            ws = [ref[j, here, :] for ref in (w0, w1, w2)]
            phase = p_ref[j, here, :]
            shift = a[0] * ws[0] + a[1] * ws[1] + a[2] * ws[2]
            out = (-4.0 * acts[j]) * (shift * shift) * (shift + 3.0 * phase)
            v0[j, here, :] = out
            outs.append(out)
            if j < tiles - 1 and own:
                to = pl.ds(pl.multiple_of(at - 16, 8), 8)
                cols = slice(j * LANES, (j + 1) * LANES)
                first = f[0] * ws[0] + f[1] * ws[1] + f[2] * ws[2]
                section_ref[to, cols] = phase + shift
                base_ref[to, cols] = phase + first
        return add_products(sums, ((outs, outs),), None) if own else sums

    def four(i, sums):
        for u in range(4):
            sums = start(1 + 4 * i + u, True, sums)
        return sums

    start(0, False, None)
    (m0,) = lax.fori_loop(0, n // 32, four, no_sums(1, tiles))
    start(n // 8 + 1, False, None)
    write_sums([m0] + powers((v0, v1, v2), coef_ref, act_ref, side_ref), sums_ref)


def third_kernel(gathered_ref, base_ref, v0, v1, v2, updated_ref):
    n, width = base_ref.shape
    r, hess = hessenberg(gathered_ref[...])
    coefs = on_basis(r, phi_column(hess, 1.0, 3), 32.0)
    d = [jnp.max(c) for c in coefs]

    def four(i, c):
        for u in range(4):
            at = pl.multiple_of(32 * i, 8) + 8 * u
            for j in range(width // LANES):
                vs = [ref[j, pl.ds(at + 16, 8), :] for ref in (v0, v1, v2)]
                cols = slice(j * LANES, (j + 1) * LANES)
                updated_ref[pl.ds(at, 8), cols] = base_ref[pl.ds(at, 8), cols] + (
                    d[0] * vs[0] + d[1] * vs[1] + d[2] * vs[2]
                )
        return c

    lax.fori_loop(0, n // 32, four, 0)


def params(mib):
    return pltpu.CompilerParams(vmem_limit_bytes=mib << 20)


VM = pl.BlockSpec(memory_space=pltpu.VMEM)
SM = pl.BlockSpec(memory_space=pltpu.SMEM)
HB = pl.BlockSpec(memory_space=pltpu.HBM)


def in_pairs(near, far, axis):
    size = lax.axis_size(axis)
    odd = [(i, ((i + 1) ^ 1) - 1) for i in range(1, size - 1)]
    return lax.ppermute(near, axis, [(i, i ^ 1) for i in range(size)]), lax.ppermute(far, axis, odd)


def total(sums):
    size = sums.shape[0]
    sent = lax.all_to_all(sums.reshape(size, 1, LANES), ALL, 0, 0, tiled=True)
    return sent.reshape(size, LANES)


def body(phase, tile_mask):
    n, width = phase.shape
    f32 = jnp.float32
    sd = jax.ShapeDtypeStruct
    odd = jnp.stack([lax.axis_index(ROW) % 2, lax.axis_index(COL) % 2]).astype(jnp.int32)
    edge = sd((8, width + LANES), f32)
    near, far = pl.pallas_call(
        strips_kernel,
        in_specs=[SM, HB, HB],
        out_specs=[VM] * 2,
        out_shape=[sd((8, n + LANES), f32)] * 2,
        scratch_shapes=[
            pltpu.VMEM((n, LANES), f32),
            pltpu.VMEM((n, LANES), f32),
            pltpu.SMEM(tile_mask.shape, jnp.int32),
            pltpu.SemaphoreType.DMA((3,)),
        ],
        compiler_params=params(4),
        name="strips",
    )(odd, phase, tile_mask)
    near, far = in_pairs(near, far, COL)
    side, near, far, masks = pl.pallas_call(
        corners_kernel,
        in_specs=[SM, VM, VM, VM, SM],
        out_specs=[VM] * 4,
        out_shape=[sd((n, LANES), f32), edge, edge, sd((2, 8, LANES), f32)],
        compiler_params=params(6),
        name="corners",
    )(odd, near, far, phase, tile_mask)
    near, far = in_pairs(near, far, ROW)
    devices = 1
    for axis in ALL:
        devices *= lax.axis_size(axis)
    tiles = width // LANES + 1
    ext = sd((tiles, n + 32, LANES), f32)
    act = sd((tiles, 8 * (tile_mask.shape[0] + 2), LANES), f32)
    scratch = [pltpu.VMEM((tiles, n + 32, LANES), f32)]
    sums = sd((devices, LANES), f32)
    p, w0, w1, w2, coef, act, part = pl.pallas_call(
        first_kernel,
        in_specs=[SM] + [VM] * 5 + [SM],
        out_specs=[VM] * 7,
        scratch_shapes=scratch,
        out_shape=[ext, ext, ext, ext, ext, act, sums],
        compiler_params=params(22),
        name="first",
    )(odd, phase, side, near, far, masks, tile_mask)
    own = sd((n, width), f32)
    section, base, v0, v1, v2, part = pl.pallas_call(
        second_kernel,
        in_specs=[VM] * 7,
        out_specs=[VM] * 6,
        scratch_shapes=scratch,
        out_shape=[own, own, ext, ext, ext, sums],
        compiler_params=params(26),
        name="second",
    )(total(part), p, w0, w1, w2, coef, act)
    updated = pl.pallas_call(
        third_kernel,
        in_specs=[VM] * 5,
        out_specs=VM,
        out_shape=own,
        compiler_params=params(12),
        name="third",
    )(total(part), base, v0, v1, v2)
    return updated, section


def solution(mesh):
    split = Mesh(mesh.devices.reshape(4, 4, 4, 2), ALL)
    in_specs = (P(ROW, COL), P(ROW, COL))
    out_specs = (P(ROW, COL), P(ROW, COL))
    return jax.shard_map(body, mesh=split, in_specs=in_specs, out_specs=out_specs, check_vma=False)
```

time: 74.8 us -> 68.4 us (0.914)
  blocking collectives: 34.6 us -> 38.9 us
  starting transfers between devices: 11.3 us -> 7.07 us
  waiting for transfers between devices: 6.36 us -> 2.17 us
  Pallas kernels: 19.7 us -> 16.6 us
    all_to_all x2, blocking collectives: 34.6 us -> 38.9 us  [total(): sent = lax.all_to_all(sums.reshape(size, 1, LANES), ALL, 0, 0, tiled=True)]
    ppermute x4, starting transfers between devices: 11.3 us -> 7.07 us  [the longest x2 4.21 us: in_pairs(): lax.ppermute(far, axis, odd)]
    ppermute x4, waiting for transfers between devices: 6.36 us -> 2.17 us  [the longest x2 1.52 us: in_pairs(): lax.ppermute(far, axis, odd)]
    pallas_call x4, Pallas kernels: 18 us -> 14.9 us  [the longest x1 6.49 us: body(): pl.pallas_call(second_kernel, in_specs=[VM] * 7, out_specs=[VM] * 6, scra...]
    unnamed x8 -> x10, local copies, waits for them, and re-layouts: 1.9 us -> 2.59 us
where the time goes in v1:
time: 68.4 us; the launch traced here: 68.2 us
  blocking collectives  38.9 us (57%)
  Pallas kernels  16.6 us (24%)
  starting transfers between devices  7.07 us (10%)
  local copies, waits for them, and re-layouts  2.59 us (4%)
  waiting for transfers between devices  2.17 us (3%)
  between operations  0.71 us (1%)
    all_to_all x2, blocking collectives, total(): sent = lax.all_to_all(sums.reshape(size, 1, LANES), ALL, 0, 0, tiled=True)  38.9 us
    pallas_call x1, Pallas kernels, body(): pl.pallas_call(second_kernel, in_specs=[VM] * 7, out_specs=[VM] * 6, scra...  6.49 us
    pallas_call x1, Pallas kernels, body(): pl.pallas_call(first_kernel, in_specs=[SM] + [VM] * 5 + [SM], out_specs=[...  6.28 us
    ppermute x2, starting transfers between devices, in_pairs(): lax.ppermute(far, axis, odd)  4.21 us
    ppermute x2, starting transfers between devices, in_pairs(): lax.ppermute(near, axis, [(i, i ^ 1) for i in range(size)])  2.86 us
    unnamed x10, local copies, waits for them, and re-layouts  2.59 us
    pallas_call x1, Pallas kernels, body(): pl.pallas_call(third_kernel, in_specs=[VM] * 5, out_specs=VM, out_shape=o...  1.76 us
    ppermute x2, waiting for transfers between devices, in_pairs(): lax.ppermute(far, axis, odd)  1.52 us
  transfers between devices with their start and end apart: 4, of which 2 were waited for; matrix products, arithmetic and copies ran while one was open for 0% of the time, Pallas kernels for 0%

profile of v1, /device:TPU:1, one launch (start us, length us, event | category | flops | bytes accessed | tf_op | source)
XLA Modules:
  0.0 68.2 jit_solution(2473844314812494125)
XLA Ops:
  0.6 0.0 copy-start.4
  0.7 0.1 pad_add_fusion.odd_ref
  0.7 0.0 copy-start
  0.7 1.2 %copy-done = f32[512,512]{1,0:T(8,128)S(1)} copy-done((f32[512,512]{1,0:T(8,128)S(1)}, f32[512,512]{1,0:T(8,128)}, u32[]{:S(2)}) %copy-start) | copy-done | bytes 1048600
  2.0 0.0 copy-start.2
  2.0 0.7 copy-done.2
  2.6 0.0 copy-start.1
  2.6 1.4 %strips.1 = (f32[8,640]{1,0:T(8,128)S(1)}, f32[8,640]{1,0:T(8,128)S(1)}) custom-call(s32[2]{0:T(128)S(1)} %pad_add_fusion.odd_ref, f32[512,512]{1,0:T(8,128)S(1)} %copy-done, s32[2,2]{1,0:T(2,128)S(1)} %copy-done.2), custom_call_target="tpu_custom_call" | custom-call | tf_op jit(solution)/shard_map/strips/pallas_call | solution.py:436
  4.0 1.5 %collective-permute-start = (f32[8,640]{1,0:T(8,128)S(1)}, f32[8,640]{1,0:T(8,128)S(1)}, u32[]{:S(2)}, u32[]{:S(2)}) collective-permute-start(f32[8,640]{1,0:T(8,128)S(1)} %get-tuple-element.21), channel_id=1, source_target_pairs={{0,1},{1,0},{2,3},{3,2},{4,5},{5,4},{6,7},{7,6},{8,9},{9,8},{10,11... | collective-permute-start | bytes 61448 | tf_op jit(solution)/shard_map/ppermute | solution.py:421
  5.5 3.6 %collective-permute-start.1 = (f32[8,640]{1,0:T(8,128)S(1)}, f32[8,640]{1,0:T(8,128)S(1)}, u32[]{:S(2)}, u32[]{:S(2)}) collective-permute-start(f32[8,640]{1,0:T(8,128)S(1)} %get-tuple-element.22), channel_id=1, source_target_pairs={{1,2},{2,1},{3,4},{4,3},{5,6},{6,5},{9,10},{10,9},{11,12},{12,11},... | collective-permute-start | bytes 61448 | tf_op jit(solution)/shard_map/ppermute | solution.py:421
  9.1 0.0 collective-permute-done.near_in
  9.1 1.5 %collective-permute-done.1.far_in = f32[8,640]{1,0:T(8,128)S(1)} collective-permute-done((f32[8,640]{1,0:T(8,128)S(1)}, f32[8,640]{1,0:T(8,128)S(1)}, u32[]{:S(2)}, u32[]{:S(2)}) %collective-permute-start.1) | collective-permute-done | bytes 20512 | tf_op jit(solution)/shard_map/ppermute | solution.py:421
  10.6 0.0 copy-done.1
  10.6 0.0 copy-start.3
  10.6 0.7 copy-done.3
  11.3 0.7 %corners.1 = (f32[512,128]{1,0:T(8,128)S(1)}, f32[8,640]{1,0:T(8,128)S(1)}, f32[8,640]{1,0:T(8,128)S(1)}, f32[2,8,128]{2,1,0:T(8,128)S(1)}) custom-call(s32[2]{0:T(128)S(1)} %pad_add_fusion.odd_ref, f32[8,640]{1,0:T(8,128)S(1)} %collective-permute-done.near_in, f32[8,640]{1,0:T(8,128)S(1)} %collective-permute-done.1.far_in, f32[512,512]{1,0:T(8,128)S(1)} %copy-done.1, ...), custom_call_target="tpu_custom_call" | custom-call | tf_op jit(solution)/shard_map/corners/pallas_call | solution.py:451
  12.0 1.4 %collective-permute-start.2 = (f32[8,640]{1,0:T(8,128)S(1)}, f32[8,640]{1,0:T(8,128)S(1)}, u32[]{:S(2)}, u32[]{:S(2)}) collective-permute-start(f32[8,640]{1,0:T(8,128)S(1)} %get-tuple-element.24), channel_id=1, source_target_pairs={{0,8},{8,0},{16,24},{24,16},{32,40},{40,32},{48,56},{56,48},{64,72... | collective-permute-start | bytes 61448 | tf_op jit(solution)/shard_map/ppermute | solution.py:421
  13.4 0.7 collective-permute-start.3
  14.1 0.7 collective-permute-done.2.near_in
  14.7 0.0 collective-permute-done.3.far_in
  14.7 0.0 copy-done.4
  14.7 6.3 %first.1 = (f32[5,544,128]{2,1,0:T(8,128)S(1)}, f32[5,544,128]{2,1,0:T(8,128)S(1)}, f32[5,544,128]{2,1,0:T(8,128)S(1)}, f32[5,544,128]{2,1,0:T(8,128)S(1)}, f32[...) custom-call(s32[2]{0:T(128)S(1)} %pad_add_fusion.odd_ref, f32[512,512]{1,0:T(8,128)S(1)} %copy-done.1, ...), custom_call_target="tpu_custom_call" | custom-call | tf_op jit(solution)/shard_map/first/pallas_call | solution.py:468
  21.0 25.1 %all_to_all.10 = f32[128,1,128]{2,1,0:T(1,128)S(1)} all-to-all(f32[128,1,128]{2,1,0:T(1,128)S(1)} %bitcast.13), channel_id=1, replica_groups=mesh['row_0'=4,'row_1'=4,'col_0'=4,'col_1'=2] {'row_0','row_1','col_0','..., dimensions={0} | all-to-all | bytes 131072 | tf_op jit(solution)/shard_map/all_to_all | solution.py:426
  46.1 6.5 %second.1 = (f32[512,512]{1,0:T(8,128)}, f32[512,512]{1,0:T(8,128)S(1)}, f32[5,544,128]{2,1,0:T(8,128)S(1)}, f32[5,544,128]{2,1,0:T(8,128)S(1)}, f32[5,544,128]{2,1,0:T(8,128)S(1)}, /*index=5*/f32[128,128]{1,0:T(8,128)S(1)}) custom-call(f32[128,128]{1,0:T(8,128)S(1)} %bitcast.10, f32[5,544,128]{2,1,0:T(8,128)S(1)} %get-tuple-element.28.p_ref, ...), custom_call_target="tpu_custom_call" | custom-call | tf_op jit(solution)/shard_map/second/pallas_call | solution.py:478
  52.6 13.8 %all_to_all.11 = f32[128,1,128]{2,1,0:T(1,128)S(1)} all-to-all(f32[128,1,128]{2,1,0:T(1,128)S(1)} %bitcast.12), channel_id=1, replica_groups=mesh['row_0'=4,'row_1'=4,'col_0'=4,'col_1'=2] {'row_0','row_1','col_0','..., dimensions={0} | all-to-all | bytes 131072 | tf_op jit(solution)/shard_map/all_to_all | solution.py:426
  66.4 1.8 %third.1 = f32[512,512]{1,0:T(8,128)} custom-call(f32[128,128]{1,0:T(8,128)S(1)} %bitcast.11, f32[512,512]{1,0:T(8,128)S(1)} %get-tuple-element.35.base_ref, f32[5,544,128]{2,1,0:T(8,128)S(1)} %get-tuple-element.36.v0, f32[5,544,128]{2,1,0:T(8,128)S(1)} %get-tuple-element.37.v1, f32[5,544,128]{2,1,0:T(8,128)S(1)} %get-tuple-element.38.v2), custom_call_target="tpu_custom_call" | custom-call | tf_op jit(solution)/shard_map/third/pallas_call | solution.py:487
Async XLA Ops:
  0.6 14.1 %copy-start.4 = (s32[2,2]{1,0:T(2,128)S(1)}, s32[2,2]{1,0:T(2,128)}, u32[]{:S(2)}) copy-start(s32[2,2]{1,0:T(2,128)} %mask_ref.3) | copy-start | bytes 52
  0.7 1.2 %copy-start = (f32[512,512]{1,0:T(8,128)S(1)}, f32[512,512]{1,0:T(8,128)}, u32[]{:S(2)}) copy-start(f32[512,512]{1,0:T(8,128)} %phase_ref.3) | copy-start | bytes 3145732
  2.0 0.7 copy-start.2
  2.6 8.0 %copy-start.1 = (f32[512,512]{1,0:T(8,128)S(1)}, f32[512,512]{1,0:T(8,128)}, u32[]{:S(2)}) copy-start(f32[512,512]{1,0:T(8,128)} %phase_ref.3) | copy-start | bytes 3145732
  4.0 5.0 %collective-permute-start = (f32[8,640]{1,0:T(8,128)S(1)}, f32[8,640]{1,0:T(8,128)S(1)}, u32[]{:S(2)}, u32[]{:S(2)}) collective-permute-start(f32[8,640]{1,0:T(8,128)S(1)} %get-tuple-element.21), channel_id=1, source_target_pairs={{0,1},{1,0},{2,3},{3,2},{4,5},{5,4},{6,7},{7,6},{8,9},{9,8},{10,11... | collective-permute-start | bytes 61448 | tf_op jit(solution)/shard_map/ppermute | solution.py:421
  5.5 5.1 %collective-permute-start.1 = (f32[8,640]{1,0:T(8,128)S(1)}, f32[8,640]{1,0:T(8,128)S(1)}, u32[]{:S(2)}, u32[]{:S(2)}) collective-permute-start(f32[8,640]{1,0:T(8,128)S(1)} %get-tuple-element.22), channel_id=1, source_target_pairs={{1,2},{2,1},{3,4},{4,3},{5,6},{6,5},{9,10},{10,9},{11,12},{12,11},... | collective-permute-start | bytes 61448 | tf_op jit(solution)/shard_map/ppermute | solution.py:421
  10.6 0.7 copy-start.3
  12.0 2.7 %collective-permute-start.2 = (f32[8,640]{1,0:T(8,128)S(1)}, f32[8,640]{1,0:T(8,128)S(1)}, u32[]{:S(2)}, u32[]{:S(2)}) collective-permute-start(f32[8,640]{1,0:T(8,128)S(1)} %get-tuple-element.24), channel_id=1, source_target_pairs={{0,8},{8,0},{16,24},{24,16},{32,40},{40,32},{48,56},{56,48},{64,72... | collective-permute-start | bytes 61448 | tf_op jit(solution)/shard_map/ppermute | solution.py:421
  13.4 1.3 %collective-permute-start.3 = (f32[8,640]{1,0:T(8,128)S(1)}, f32[8,640]{1,0:T(8,128)S(1)}, u32[]{:S(2)}, u32[]{:S(2)}) collective-permute-start(f32[8,640]{1,0:T(8,128)S(1)} %get-tuple-element.25), channel_id=1, source_target_pairs={{8,16},{16,8},{24,32},{32,24},{40,48},{48,40},{56,64},{64,56},{72,... | collective-permute-start | bytes 61448 | tf_op jit(solution)/shard_map/ppermute | solution.py:421

commit v2 on v1

--- a/solution.py
+++ b/solution.py
@@ -14,7 +14,7 @@
 ALL = ROW + COL
 HALO = 8
 LANES = 128
-UNROLL = 11
+UNROLL = 33
 
 
 def splat(row, lane, k):
@@ -138,28 +138,14 @@
         unroll -= 1
     steps = groups // unroll
 
-    def ahead(group, at):
-        for u in range(unroll):
-            for j, v in enumerate(beside(src, at + 8 * u, sides)):
-                side_ref[j, pl.ds(at + 8 * u, 8), :] = v
-
-    def here(group, at, c):
-        for u in range(unroll):
-            side = [side_ref[j, pl.ds(at + 8 * u, 8), :] for j in range(src.shape[0])]
-            c = emit(group + u, at + 8 * u, side, u, c)
-        return c
-
-    def both(i, c):
+    def step(i, c):
         group = first + i * unroll
         at = pl.multiple_of(8 + 8 * group, 8)
-        c = here(group, at, c)
-        ahead(group + unroll, at + 8 * unroll)
+        for u in range(unroll):
+            c = emit(group + u, at + 8 * u, beside(src, at + 8 * u, sides), u, c)
         return c
 
-    ahead(first, 8 + 8 * first)
-    carry = lax.fori_loop(0, steps - 1, both, carry)
-    group = first + (steps - 1) * unroll
-    return here(group, 8 + 8 * group, carry)
+    return lax.fori_loop(0, steps, step, carry)
 
 
 def add_products(sums, pairs, own):

time: 68.4 us -> 64.2 us (0.939)
  Pallas kernels: 16.6 us -> 12.5 us
    pallas_call x1, Pallas kernels: 6.28 us -> 4.16 us  [body(): pl.pallas_call(first_kernel, in_specs=[SM] + [VM] * 5 + [SM], out_specs=[...]
    pallas_call x1, Pallas kernels: 6.49 us -> 4.47 us  [body(): pl.pallas_call(second_kernel, in_specs=[VM] * 7, out_specs=[VM] * 6, scra...]
where the time goes in v2:
time: 64.2 us; the launch traced here: 64 us
  blocking collectives  38.9 us (61%)
  Pallas kernels  12.5 us (19%)
  starting transfers between devices  7.07 us (11%)
  local copies, waits for them, and re-layouts  2.59 us (4%)
  waiting for transfers between devices  2.17 us (3%)
  between operations  0.71 us (1%)
    all_to_all x2, blocking collectives, total(): sent = lax.all_to_all(sums.reshape(size, 1, LANES), ALL, 0, 0, tiled=True)  38.9 us
    pallas_call x1, Pallas kernels, body(): pl.pallas_call(second_kernel, in_specs=[VM] * 7, out_specs=[VM] * 6, scra...  4.47 us
    ppermute x2, starting transfers between devices, in_pairs(): lax.ppermute(far, axis, odd)  4.21 us
    pallas_call x1, Pallas kernels, body(): pl.pallas_call(first_kernel, in_specs=[SM] + [VM] * 5 + [SM], out_specs=[...  4.16 us
    ppermute x2, starting transfers between devices, in_pairs(): lax.ppermute(near, axis, [(i, i ^ 1) for i in range(size)])  2.86 us
    unnamed x10, local copies, waits for them, and re-layouts  2.59 us
    pallas_call x1, Pallas kernels, body(): pl.pallas_call(third_kernel, in_specs=[VM] * 5, out_specs=VM, out_shape=o...  1.76 us
    ppermute x2, waiting for transfers between devices, in_pairs(): lax.ppermute(far, axis, odd)  1.52 us
  transfers between devices with their start and end apart: 4, of which 2 were waited for; matrix products, arithmetic and copies ran while one was open for 0% of the time, Pallas kernels for 0%

profile of v2, /device:TPU:1, one launch (start us, length us, event | category | flops | bytes accessed | tf_op | source)
XLA Modules:
  0.0 64.0 jit_solution(3473768413151370509)
XLA Ops:
  0.6 0.0 copy-start.4
  0.7 0.1 pad_add_fusion.odd_ref
  0.7 0.0 copy-start
  0.7 1.2 %copy-done = f32[512,512]{1,0:T(8,128)S(1)} copy-done((f32[512,512]{1,0:T(8,128)S(1)}, f32[512,512]{1,0:T(8,128)}, u32[]{:S(2)}) %copy-start) | copy-done | bytes 1048600
  2.0 0.0 copy-start.2
  2.0 0.7 %copy-done.2 = s32[2,2]{1,0:T(2,128)S(1)} copy-done((s32[2,2]{1,0:T(2,128)S(1)}, s32[2,2]{1,0:T(2,128)}, u32[]{:S(2)}) %copy-start.2) | copy-done | bytes 40
  2.6 0.0 copy-start.1
  2.6 1.4 %strips.1 = (f32[8,640]{1,0:T(8,128)S(1)}, f32[8,640]{1,0:T(8,128)S(1)}) custom-call(s32[2]{0:T(128)S(1)} %pad_add_fusion.odd_ref, f32[512,512]{1,0:T(8,128)S(1)} %copy-done, s32[2,2]{1,0:T(2,128)S(1)} %copy-done.2), custom_call_target="tpu_custom_call" | custom-call | tf_op jit(solution)/shard_map/strips/pallas_call | solution.py:422
  4.0 1.5 %collective-permute-start = (f32[8,640]{1,0:T(8,128)S(1)}, f32[8,640]{1,0:T(8,128)S(1)}, u32[]{:S(2)}, u32[]{:S(2)}) collective-permute-start(f32[8,640]{1,0:T(8,128)S(1)} %get-tuple-element.21), channel_id=1, source_target_pairs={{0,1},{1,0},{2,3},{3,2},{4,5},{5,4},{6,7},{7,6},{8,9},{9,8},{10,11... | collective-permute-start | bytes 61448 | tf_op jit(solution)/shard_map/ppermute | solution.py:407
  5.5 3.6 %collective-permute-start.1 = (f32[8,640]{1,0:T(8,128)S(1)}, f32[8,640]{1,0:T(8,128)S(1)}, u32[]{:S(2)}, u32[]{:S(2)}) collective-permute-start(f32[8,640]{1,0:T(8,128)S(1)} %get-tuple-element.22), channel_id=1, source_target_pairs={{1,2},{2,1},{3,4},{4,3},{5,6},{6,5},{9,10},{10,9},{11,12},{12,11},... | collective-permute-start | bytes 61448 | tf_op jit(solution)/shard_map/ppermute | solution.py:407
  9.1 0.0 collective-permute-done.near_in
  9.1 1.5 %collective-permute-done.1.far_in = f32[8,640]{1,0:T(8,128)S(1)} collective-permute-done((f32[8,640]{1,0:T(8,128)S(1)}, f32[8,640]{1,0:T(8,128)S(1)}, u32[]{:S(2)}, u32[]{:S(2)}) %collective-permute-start.1) | collective-permute-done | bytes 20512 | tf_op jit(solution)/shard_map/ppermute | solution.py:407
  10.6 0.0 copy-done.1
  10.6 0.0 copy-start.3
  10.6 0.7 %copy-done.3 = s32[2,2]{1,0:T(2,128)S(1)} copy-done((s32[2,2]{1,0:T(2,128)S(1)}, s32[2,2]{1,0:T(2,128)}, u32[]{:S(2)}) %copy-start.3) | copy-done | bytes 40
  11.3 0.7 %corners.1 = (f32[512,128]{1,0:T(8,128)S(1)}, f32[8,640]{1,0:T(8,128)S(1)}, f32[8,640]{1,0:T(8,128)S(1)}, f32[2,8,128]{2,1,0:T(8,128)S(1)}) custom-call(s32[2]{0:T(128)S(1)} %pad_add_fusion.odd_ref, f32[8,640]{1,0:T(8,128)S(1)} %collective-permute-done.near_in, f32[8,640]{1,0:T(8,128)S(1)} %collective-permute-done.1.far_in, f32[512,512]{1,0:T(8,128)S(1)} %copy-done.1, ...), custom_call_target="tpu_custom_call" | custom-call | tf_op jit(solution)/shard_map/corners/pallas_call | solution.py:437
  12.0 1.4 %collective-permute-start.2 = (f32[8,640]{1,0:T(8,128)S(1)}, f32[8,640]{1,0:T(8,128)S(1)}, u32[]{:S(2)}, u32[]{:S(2)}) collective-permute-start(f32[8,640]{1,0:T(8,128)S(1)} %get-tuple-element.24), channel_id=1, source_target_pairs={{0,8},{8,0},{16,24},{24,16},{32,40},{40,32},{48,56},{56,48},{64,72... | collective-permute-start | bytes 61448 | tf_op jit(solution)/shard_map/ppermute | solution.py:407
  13.4 0.7 %collective-permute-start.3 = (f32[8,640]{1,0:T(8,128)S(1)}, f32[8,640]{1,0:T(8,128)S(1)}, u32[]{:S(2)}, u32[]{:S(2)}) collective-permute-start(f32[8,640]{1,0:T(8,128)S(1)} %get-tuple-element.25), channel_id=1, source_target_pairs={{8,16},{16,8},{24,32},{32,24},{40,48},{48,40},{56,64},{64,56},{72,... | collective-permute-start | bytes 61448 | tf_op jit(solution)/shard_map/ppermute | solution.py:407
  14.1 0.7 %collective-permute-done.2.near_in = f32[8,640]{1,0:T(8,128)S(1)} collective-permute-done((f32[8,640]{1,0:T(8,128)S(1)}, f32[8,640]{1,0:T(8,128)S(1)}, u32[]{:S(2)}, u32[]{:S(2)}) %collective-permute-start.2) | collective-permute-done | bytes 20512 | tf_op jit(solution)/shard_map/ppermute | solution.py:407
  14.7 0.0 collective-permute-done.3.far_in
  14.7 0.0 copy-done.4
  14.7 4.2 %first.1 = (f32[5,544,128]{2,1,0:T(8,128)S(1)}, f32[5,544,128]{2,1,0:T(8,128)S(1)}, f32[5,544,128]{2,1,0:T(8,128)S(1)}, f32[5,544,128]{2,1,0:T(8,128)S(1)}, f32[...) custom-call(s32[2]{0:T(128)S(1)} %pad_add_fusion.odd_ref, f32[512,512]{1,0:T(8,128)S(1)} %copy-done.1, ...), custom_call_target="tpu_custom_call" | custom-call | tf_op jit(solution)/shard_map/first/pallas_call | solution.py:454
  18.9 25.1 %all_to_all.10 = f32[128,1,128]{2,1,0:T(1,128)S(1)} all-to-all(f32[128,1,128]{2,1,0:T(1,128)S(1)} %bitcast.13), channel_id=1, replica_groups=mesh['row_0'=4,'row_1'=4,'col_0'=4,'col_1'=2] {'row_0','row_1','col_0','..., dimensions={0} | all-to-all | bytes 131072 | tf_op jit(solution)/shard_map/all_to_all | solution.py:412
  44.0 4.5 %second.1 = (f32[512,512]{1,0:T(8,128)}, f32[512,512]{1,0:T(8,128)S(1)}, f32[5,544,128]{2,1,0:T(8,128)S(1)}, f32[5,544,128]{2,1,0:T(8,128)S(1)}, f32[5,544,128]{2,1,0:T(8,128)S(1)}, /*index=5*/f32[128,128]{1,0:T(8,128)S(1)}) custom-call(f32[128,128]{1,0:T(8,128)S(1)} %bitcast.10, f32[5,544,128]{2,1,0:T(8,128)S(1)} %get-tuple-element.28.p_ref, ...), custom_call_target="tpu_custom_call" | custom-call | tf_op jit(solution)/shard_map/second/pallas_call | solution.py:464
  48.4 13.8 %all_to_all.11 = f32[128,1,128]{2,1,0:T(1,128)S(1)} all-to-all(f32[128,1,128]{2,1,0:T(1,128)S(1)} %bitcast.12), channel_id=1, replica_groups=mesh['row_0'=4,'row_1'=4,'col_0'=4,'col_1'=2] {'row_0','row_1','col_0','..., dimensions={0} | all-to-all | bytes 131072 | tf_op jit(solution)/shard_map/all_to_all | solution.py:412
  62.3 1.8 %third.1 = f32[512,512]{1,0:T(8,128)} custom-call(f32[128,128]{1,0:T(8,128)S(1)} %bitcast.11, f32[512,512]{1,0:T(8,128)S(1)} %get-tuple-element.35.base_ref, f32[5,544,128]{2,1,0:T(8,128)S(1)} %get-tuple-element.36.v0, f32[5,544,128]{2,1,0:T(8,128)S(1)} %get-tuple-element.37.v1, f32[5,544,128]{2,1,0:T(8,128)S(1)} %get-tuple-element.38.v2), custom_call_target="tpu_custom_call" | custom-call | tf_op jit(solution)/shard_map/third/pallas_call | solution.py:473
Async XLA Ops:
  0.6 14.1 %copy-start.4 = (s32[2,2]{1,0:T(2,128)S(1)}, s32[2,2]{1,0:T(2,128)}, u32[]{:S(2)}) copy-start(s32[2,2]{1,0:T(2,128)} %mask_ref.3) | copy-start | bytes 52
  0.7 1.2 %copy-start = (f32[512,512]{1,0:T(8,128)S(1)}, f32[512,512]{1,0:T(8,128)}, u32[]{:S(2)}) copy-start(f32[512,512]{1,0:T(8,128)} %phase_ref.3) | copy-start | bytes 3145732
  2.0 0.7 %copy-start.2 = (s32[2,2]{1,0:T(2,128)S(1)}, s32[2,2]{1,0:T(2,128)}, u32[]{:S(2)}) copy-start(s32[2,2]{1,0:T(2,128)} %mask_ref.3) | copy-start | bytes 52
  2.6 8.0 %copy-start.1 = (f32[512,512]{1,0:T(8,128)S(1)}, f32[512,512]{1,0:T(8,128)}, u32[]{:S(2)}) copy-start(f32[512,512]{1,0:T(8,128)} %phase_ref.3) | copy-start | bytes 3145732
  4.0 5.0 %collective-permute-start = (f32[8,640]{1,0:T(8,128)S(1)}, f32[8,640]{1,0:T(8,128)S(1)}, u32[]{:S(2)}, u32[]{:S(2)}) collective-permute-start(f32[8,640]{1,0:T(8,128)S(1)} %get-tuple-element.21), channel_id=1, source_target_pairs={{0,1},{1,0},{2,3},{3,2},{4,5},{5,4},{6,7},{7,6},{8,9},{9,8},{10,11... | collective-permute-start | bytes 61448 | tf_op jit(solution)/shard_map/ppermute | solution.py:407
  5.5 5.1 %collective-permute-start.1 = (f32[8,640]{1,0:T(8,128)S(1)}, f32[8,640]{1,0:T(8,128)S(1)}, u32[]{:S(2)}, u32[]{:S(2)}) collective-permute-start(f32[8,640]{1,0:T(8,128)S(1)} %get-tuple-element.22), channel_id=1, source_target_pairs={{1,2},{2,1},{3,4},{4,3},{5,6},{6,5},{9,10},{10,9},{11,12},{12,11},... | collective-permute-start | bytes 61448 | tf_op jit(solution)/shard_map/ppermute | solution.py:407
  10.6 0.7 %copy-start.3 = (s32[2,2]{1,0:T(2,128)S(1)}, s32[2,2]{1,0:T(2,128)}, u32[]{:S(2)}) copy-start(s32[2,2]{1,0:T(2,128)} %mask_ref.3) | copy-start | bytes 52
  12.0 2.7 %collective-permute-start.2 = (f32[8,640]{1,0:T(8,128)S(1)}, f32[8,640]{1,0:T(8,128)S(1)}, u32[]{:S(2)}, u32[]{:S(2)}) collective-permute-start(f32[8,640]{1,0:T(8,128)S(1)} %get-tuple-element.24), channel_id=1, source_target_pairs={{0,8},{8,0},{16,24},{24,16},{32,40},{40,32},{48,56},{56,48},{64,72... | collective-permute-start | bytes 61448 | tf_op jit(solution)/shard_map/ppermute | solution.py:407
  13.4 1.3 %collective-permute-start.3 = (f32[8,640]{1,0:T(8,128)S(1)}, f32[8,640]{1,0:T(8,128)S(1)}, u32[]{:S(2)}, u32[]{:S(2)}) collective-permute-start(f32[8,640]{1,0:T(8,128)S(1)} %get-tuple-element.25), channel_id=1, source_target_pairs={{8,16},{16,8},{24,32},{32,24},{40,48},{48,40},{56,64},{64,56},{72,... | collective-permute-start | bytes 61448 | tf_op jit(solution)/shard_map/ppermute | solution.py:407

commit v3 on v2

v3 whole, which is shorter than its diff:
```python
import functools

import jax
import jax.numpy as jnp
from jax import lax
from jax.experimental import pallas as pl
from jax.experimental.pallas import tpu as pltpu
from jax.sharding import Mesh
from jax.sharding import PartitionSpec as P

TILE = 256
ROW = ("row_0", "row_1")
COL = ("col_0", "col_1")
ALL = ROW + COL
HALO = 8
LANES = 128
UNROLL = 33
CHUNKS = 4


def splat(row, lane, k):
    return jnp.broadcast_to(
        jnp.sum(jnp.where(lane == k, row, 0.0), axis=1, keepdims=True), (8, LANES)
    )


def matmul3(a, b):
    return [
        [a[i][0] * b[0][j] + a[i][1] * b[1][j] + a[i][2] * b[2][j] for j in range(3)]
        for i in range(3)
    ]


def phi_column(hess, scale, order):
    inv = 1.0 / 1024.0
    base = [[hess[i][j] * (scale * inv) for j in range(3)] for i in range(3)]
    zero = jnp.zeros((8, LANES), jnp.float32)
    term = base
    cols = [[zero + inv, zero, zero]] + [[zero] * 3 for _ in range(order - 1)]
    total = base
    sums = cols
    for degree in range(2, 11):
        first = [term[i][0] * (inv / degree) for i in range(3)]
        cols = [first] + [[c * (inv / degree) for c in col] for col in cols[:-1]]
        term = [[v * (1.0 / degree) for v in row] for row in matmul3(term, base)]
        total = [[total[i][j] + term[i][j] for j in range(3)] for i in range(3)]
        sums = [[s + c for s, c in zip(sc, cc)] for sc, cc in zip(sums, cols)]
    one, two = inv, 0.5 * inv * inv
    for _ in range(10):
        moved = []
        for n, col in enumerate(sums):
            new = [
                2.0 * col[i]
                + (total[i][0] * col[0] + total[i][1] * col[1] + total[i][2] * col[2])
                for i in range(3)
            ]
            if n >= 1:
                new = [new[i] + sums[n - 1][i] * one for i in range(3)]
            if n >= 2:
                new = [new[i] + sums[n - 2][i] * two for i in range(3)]
            moved.append(new)
        square = matmul3(total, total)
        total = [[2.0 * total[i][j] + square[i][j] for j in range(3)] for i in range(3)]
        sums = moved
        one, two = 2.0 * one, 2.0 * two + one * one
    return sums[-1]


def root(x):
    inv = lax.rsqrt(x)
    inv = inv * (1.5 - 0.5 * (x * inv) * inv)
    return x * inv, inv


def hessenberg(gathered):
    lane = lax.broadcasted_iota(jnp.int32, (8, LANES), 1)
    row = jnp.broadcast_to(jnp.sum(gathered, axis=0, keepdims=True), (8, LANES))
    m = [splat(row, lane, n) for n in range(6)]
    r00, i0 = root(m[0])
    r01, r02, r03 = m[1] * i0, m[2] * i0, m[3] * i0
    r11, i1 = root(jnp.maximum(m[2] - r01 * r01, 1e-9 * m[2]))
    r12, r13 = (m[3] - r01 * r02) * i1, (m[4] - r01 * r03) * i1
    r22, i2 = root(jnp.maximum(m[4] - r02 * r02 - r12 * r12, 1e-9 * m[4]))
    r23 = (m[5] - r02 * r03 - r12 * r13) * i2
    zero = jnp.zeros((8, LANES), jnp.float32)
    j0, j1, j2 = 8.0 * i0, 8.0 * i1, 8.0 * i2
    c0 = [r01 * j0, r11 * j0, zero]
    d0, d1 = 0.125 * c0[0], 0.125 * c0[1]
    c1 = [(r02 - d0 * r01) * j1, (r12 - d1 * r01) * j1, r22 * j1]
    e0, e1, e2 = [0.125 * v for v in c1]
    c2 = [(r03 - d0 * r02 - e0 * r12) * j2, (r13 - d1 * r02 - e1 * r12) * j2, (r23 - e2 * r12) * j2]
    hess = [[c0[i], c1[i], c2[i]] for i in range(3)]
    for i in range(3):
        hess[i][i] = hess[i][i] - 8.0
    return (r00, r01, r02, r12, i0, i1, i2), hess


def on_basis(r, weights, factor):
    r00, r01, r02, r12, i0, i1, i2 = r
    scale = factor * r00
    d2 = weights[2] * i2
    d1 = (weights[1] - r12 * d2) * i1
    d0 = (weights[0] - r01 * d1 - r02 * d2) * i0
    return [d0 * scale, d1 * scale, d2 * scale]


def beside(ref, at, sides):
    tiles = ref.shape[0]
    lane = lax.broadcasted_iota(jnp.int32, (8, LANES), 1)
    mids = [ref[j, pl.ds(at, 8), :] for j in range(tiles)]
    ones = [pltpu.roll(m, 1, 1) for m in mids]
    out = [jnp.where(lane == 0, ones[j - 1], ones[j]) for j in range(tiles)]
    if sides == 2:
        backs = [pltpu.roll(m, LANES - 1, 1) for m in mids]
        out = [o + jnp.where(lane == LANES - 1, backs[(j + 1) % tiles], backs[j]) for j, o in enumerate(out)]
    return out


def sum_row(sums):
    sub = lax.broadcasted_iota(jnp.int32, (8, LANES), 0)
    lane = lax.broadcasted_iota(jnp.int32, (8, LANES), 1)
    rows = jnp.zeros((8, LANES), jnp.float32)
    for n, tiles in enumerate(sums):
        part = jnp.sum(sum(tiles[1:], tiles[0]), axis=0, keepdims=True)
        rows = jnp.where(sub == n, part, rows)
    values = jnp.sum(rows, axis=1, keepdims=True)
    row = jnp.sum(jnp.where(lane == sub, values, 0.0), axis=0, keepdims=True)
    return jnp.broadcast_to(row, (8, LANES))


def write_row(row, out_ref):
    for i in range(0, out_ref.shape[0], 8):
        out_ref[i : i + 8, :] = row


def band_of(group, bands):
    return jnp.clip((group - 1 + TILE // 8) // (TILE // 8), 0, bands - 1)


def act_of(act_ref, group):
    bands = act_ref.shape[1] // 8
    if isinstance(group, int):
        band = 8 * min(max((group - 1 + TILE // 8) // (TILE // 8), 0), bands - 1)
    else:
        band = pl.multiple_of(8 * band_of(group, bands), 8)
    return [act_ref[j, pl.ds(band, 8), :] for j in range(act_ref.shape[0])]


def over_groups(lo, hi, emit, carry, most=UNROLL):
    unroll = min(most, hi - lo)
    while (hi - lo) % unroll:
        unroll -= 1

    def step(i, c):
        group = lo + i * unroll
        at = pl.multiple_of(8 + 8 * group, 8)
        for u in range(unroll):
            c = emit(group + u, at + 8 * u, c)
        return c

    if hi - lo == unroll:
        for g in range(lo, hi):
            carry = emit(g, 8 + 8 * g, carry)
        return carry
    return lax.fori_loop(0, (hi - lo) // unroll, step, carry)


def is_own(group, groups):
    return not isinstance(group, int) or 0 < group < groups - 1


def add_products(sums, pairs):
    return tuple(
        tuple(s + a[j] * b[j] for j, s in enumerate(row)) for row, (a, b) in zip(sums, pairs)
    )


def no_sums(count, tiles):
    return tuple(tuple(jnp.zeros((8, LANES), jnp.float32) for _ in range(tiles - 1)) for _ in range(count))


def power_of(src, dst, coef_ref, act_ref):
    tiles, rows, _ = src.shape
    groups = (rows - 16) // 8

    def emit(group, at, sums):
        side = beside(src, at, 2)
        acts = act_of(act_ref, group)
        here = pl.ds(at, 8)
        mids, outs = [], []
        for j in range(tiles):
            mid = src[j, here, :]
            total = side[j] + (src[j, pl.ds(at - 1, 8), :] + src[j, pl.ds(at + 1, 8), :])
            out = acts[j] * total + coef_ref[j, here, :] * mid
            dst[j, here, :] = out
            mids.append(mid)
            outs.append(out)
        return add_products(sums, ((mids, outs), (outs, outs))) if is_own(group, groups) else sums

    return emit


def form_of(src, coef_ref):
    tiles = src.shape[0]

    def emit(group, at, sums):
        side = beside(src, at, 1)
        here = pl.ds(at, 8)
        mids, images = [], []
        for j in range(tiles - 1):
            mid = src[j, here, :]
            images.append(0.5 * (side[j] + src[j, pl.ds(at - 1, 8), :]) + coef_ref[j, here, :] * mid)
            mids.append(mid)
        return add_products(sums, ((mids, images),))

    return emit


def force_of(p_ref, w0, coef_ref, act_ref):
    tiles, rows, _ = p_ref.shape
    groups = (rows - 16) // 8

    def emit(group, at, sums):
        side = beside(p_ref, at, 2)
        acts = act_of(act_ref, group)
        here = pl.ds(at, 8)
        outs = []
        for j in range(tiles):
            mid = p_ref[j, here, :]
            total = side[j] + (p_ref[j, pl.ds(at - 1, 8), :] + p_ref[j, pl.ds(at + 1, 8), :])
            square = mid * mid
            out = acts[j] * (8.0 * total - (28.0 + 4.0 * square) * mid)
            w0[j, here, :] = out
            coef_ref[j, here, :] = acts[j] * (0.5 - 1.5 * square)
            outs.append(out)
        return add_products(sums, ((outs, outs),)) if is_own(group, groups) else sums

    return emit


def strips_kernel(odd_ref, phase_hbm, mask_hbm, near_ref, far_ref, own_ref, left_ref, right_ref, mask_ref, sems):
    n, width = phase_hbm.shape
    copies = [
        pltpu.make_async_copy(phase_hbm.at[:, 0:LANES], left_ref, sems.at[0]),
        pltpu.make_async_copy(phase_hbm.at[:, width - LANES : width], right_ref, sems.at[1]),
        pltpu.make_async_copy(mask_hbm, mask_ref, sems.at[2]),
    ]
    for c in copies:
        c.start()
    for c in copies:
        c.wait()
    odd = jnp.full((8, LANES), odd_ref[1], jnp.int32) > 0
    odd_n = jnp.full((8, n), odd_ref[1], jnp.int32) > 0
    lane = lax.broadcasted_iota(jnp.int32, (8, LANES), 1)
    strips = []
    for ref, rows, col in ((left_ref, 0, 0), (right_ref, LANES - 8, mask_ref.shape[1] - 1)):
        extra = jnp.zeros((8, LANES), jnp.float32)
        for t in range(mask_ref.shape[0]):
            extra = extra + jnp.where(lane == t, mask_ref[t, col].astype(jnp.float32), 0.0)
        strips.append((ref[...].T[rows : rows + 8, :], extra))
    own = jnp.zeros((8, LANES), jnp.float32)
    tiles_r, tiles_c = mask_ref.shape
    for t in range(tiles_r):
        for c in range(tiles_c):
            own = jnp.where(lane == t * tiles_c + c, mask_ref[t, c].astype(jnp.float32), own)
    own_ref[...] = own
    left, right = strips
    for out, a, b in ((near_ref, left, right), (far_ref, right, left)):
        out[:, :n] = jnp.where(odd_n, a[0], b[0])
        out[:, n:] = jnp.where(odd, a[1], b[1])


def corners_kernel(odd_ref, near_in, far_in, phase_ref, own_ref, side_ref, near_ref, far_ref, masks_ref):
    n, width = phase_ref.shape
    tiles_r, tiles_c = n // TILE, width // TILE
    odd = jnp.full((8, LANES), odd_ref[1], jnp.int32) > 0
    odd_n = jnp.full((8, n), odd_ref[1], jnp.int32) > 0
    from_left = jnp.where(odd_n, near_in[:, :n], far_in[:, :n])
    from_right = jnp.where(odd_n, far_in[:, :n], near_in[:, :n])
    mask_left = jnp.where(odd, near_in[:, n:], far_in[:, n:])
    mask_right = jnp.where(odd, far_in[:, n:], near_in[:, n:])
    masks_ref[0] = mask_left
    masks_ref[1] = mask_right
    zeros = jnp.zeros((LANES - 16, n), jnp.float32)
    side = jnp.concatenate([from_right, zeros, from_left], axis=0).T
    side_ref[...] = side
    lane = lax.broadcasted_iota(jnp.int32, (8, LANES), 1)
    strips = []
    for rows, t in ((0, 0), (n - 8, tiles_r - 1)):
        extra = side[rows : rows + 8, :]
        for c in range(tiles_c):
            extra = jnp.where(lane == 16 + c, splat(own_ref[...], lane, t * tiles_c + c), extra)
        extra = jnp.where(lane == 16 + tiles_c, splat(mask_right, lane, t), extra)
        extra = jnp.where(lane == 17 + tiles_c, splat(mask_left, lane, t), extra)
        strips.append((phase_ref[rows : rows + 8, :], extra))
    up, down = strips
    odd = jnp.full((8, LANES), odd_ref[0], jnp.int32) > 0
    odd_w = jnp.full((8, width), odd_ref[0], jnp.int32) > 0
    for out, a, b in ((near_ref, up, down), (far_ref, down, up)):
        out[:, :width] = jnp.where(odd_w, a[0], b[0])
        out[:, width:] = jnp.where(odd, a[1], b[1])


def act_cells(act_ref, band, values, right, left):
    tiles = act_ref.shape[0]
    lane = lax.broadcasted_iota(jnp.int32, (8, LANES), 1)
    for j in range(tiles - 1):
        act_ref[j, 8 * band : 8 * band + 8, :] = 0.25 * values[j * LANES // TILE]
    ends = jnp.where(lane < 8, right, jnp.where(lane >= LANES - 8, left, 0.0))
    act_ref[tiles - 1, 8 * band : 8 * band + 8, :] = 0.25 * ends


def first_passes(p_ref, w0, w1, w2, coef_ref, act_ref):
    return (
        (force_of(p_ref, w0, coef_ref, act_ref), 1),
        (power_of(w0, w1, coef_ref, act_ref), 2),
        (power_of(w1, w2, coef_ref, act_ref), 2),
        (form_of(w2, coef_ref), 1),
    )


def inner_kernel(phase_ref, side_in, masks_ref, own_ref, p_ref, w0, w1, w2, coef_ref, act_ref, sums_ref):
    n, width = phase_ref.shape
    tiles = p_ref.shape[0]
    groups = n // 8 + 2
    tiles_r, tiles_c = n // TILE, width // TILE
    lane = lax.broadcasted_iota(jnp.int32, (8, LANES), 1)
    for t in range(tiles_r):
        values = [splat(own_ref[...], lane, t * tiles_c + c) for c in range(tiles_c)]
        act_cells(act_ref, t + 1, values, splat(masks_ref[1], lane, t), splat(masks_ref[0], lane, t))
    for j in range(tiles - 1):
        p_ref[j, 16 : n + 16, :] = phase_ref[:, j * LANES : (j + 1) * LANES]
    p_ref[tiles - 1, 16 : n + 16, :] = side_in[...]
    sums = []
    for k, (emit, count) in enumerate(first_passes(p_ref, w0, w1, w2, coef_ref, act_ref)):
        sums += over_groups(2 + k, groups - 2 - k, emit, no_sums(count, tiles))
    sums_ref[...] = sum_row(sums)


def outer_kernel(
    odd_ref, near_in, far_in, inner_ref, p_in, w0_in, w1_in, w2_in, coef_in, act_in,
    p_ref, w0, w1, w2, coef_ref, act_ref, sums_ref,
):
    tiles, rows, _ = p_ref.shape
    n = rows - 32
    groups = n // 8 + 2
    width = LANES * (tiles - 1)
    tiles_r, tiles_c = n // TILE, width // TILE
    lane = lax.broadcasted_iota(jnp.int32, (8, LANES), 1)
    odd = jnp.full((8, LANES), odd_ref[0], jnp.int32) > 0
    up = [jnp.where(odd, near_in[:, j * LANES : (j + 1) * LANES], far_in[:, j * LANES : (j + 1) * LANES]) for j in range(tiles)]
    down = [jnp.where(odd, far_in[:, j * LANES : (j + 1) * LANES], near_in[:, j * LANES : (j + 1) * LANES]) for j in range(tiles)]
    for t, extra in ((0, up[-1]), (tiles_r + 1, down[-1])):
        values = [splat(extra, lane, 16 + c) for c in range(tiles_c + 2)]
        act_cells(act_ref, t, values[:tiles_c], values[tiles_c], values[tiles_c + 1])
    blank = jnp.zeros((8, LANES), jnp.float32)
    for ref in (p_ref, w0, w1, w2):
        for j in range(tiles):
            ref[j, 0:8, :] = blank
            ref[j, n + 24 : n + 32, :] = blank
    for at, strip in ((8, up), (n + 16, down)):
        for j in range(tiles - 1):
            p_ref[j, at : at + 8, :] = strip[j]
        p_ref[tiles - 1, at : at + 8, :] = jnp.where((lane < 8) | (lane >= LANES - 8), strip[-1], 0.0)
    sums = []
    for k, (emit, count) in enumerate(first_passes(p_ref, w0, w1, w2, coef_ref, act_ref)):
        own = k == 3
        part = no_sums(count, tiles)
        part = over_groups(1 if own else 0, 2 + k, emit, part)
        sums += over_groups(groups - 2 - k, groups - 1 if own else groups, emit, part)
    write_row(sum_row(sums) + inner_ref[...], sums_ref)


def second_kernel(
    gathered_ref, p_ref, w0, w1, w2, coef_ref, act_ref,
    section_hbm, base_ref, v0, v1, v2, sums_ref, section_ref, sem,
):
    tiles, rows, _ = p_ref.shape
    groups = (rows - 16) // 8
    r, hess = hessenberg(gathered_ref[...])
    a = on_basis(r, phi_column(hess, 0.5, 1), 0.5)
    f = on_basis(r, phi_column(hess, 1.0, 1), 1.0)
    blank = jnp.zeros((8, LANES), jnp.float32)
    for ref in (v0, v1, v2):
        for j in range(tiles):
            ref[j, 0:8, :] = blank
            ref[j, rows - 8 : rows, :] = blank

    def start(group, at, sums):
        acts = act_of(act_ref, group)
        here = pl.ds(at, 8)
        own = is_own(group, groups)
        outs = []
        for j in range(tiles):
            ws = [ref[j, here, :] for ref in (w0, w1, w2)]
            phase = p_ref[j, here, :]
            shift = a[0] * ws[0] + a[1] * ws[1] + a[2] * ws[2]
            out = (-4.0 * acts[j]) * (shift * shift) * (shift + 3.0 * phase)
            v0[j, here, :] = out
            outs.append(out)
            if own and j < tiles - 1:
                to = pl.ds(pl.multiple_of(at - 16, 8), 8)
                cols = slice(j * LANES, (j + 1) * LANES)
                section_ref[to, cols] = phase + shift
                base_ref[to, cols] = phase + (f[0] * ws[0] + f[1] * ws[1] + f[2] * ws[2])
        return add_products(sums, ((outs, outs),)) if own else sums

    def sides(emit, count, most):
        part = over_groups(0, 1, emit, no_sums(count, tiles))
        part = over_groups(1, groups - 1, emit, part, most)
        return over_groups(groups - 1, groups, emit, part)

    sums = [*sides(start, 1, 8)]
    copy = pltpu.make_async_copy(section_ref, section_hbm, sem)
    copy.start()
    sums += sides(power_of(v0, v1, coef_ref, act_ref), 2, UNROLL)
    sums += sides(power_of(v1, v2, coef_ref, act_ref), 2, UNROLL)
    sums += over_groups(1, groups - 1, form_of(v2, coef_ref), no_sums(1, tiles))
    write_row(sum_row(sums), sums_ref)
    copy.wait()


def third_kernel(gathered_ref, base_ref, v0, v1, v2, updated_hbm, updated_ref, sems):
    n, width = base_ref.shape
    r, hess = hessenberg(gathered_ref[...])
    d = on_basis(r, phi_column(hess, 1.0, 3), 32.0)

    def emit(group, at, c):
        here = pl.ds(at, 8)
        to = pl.ds(pl.multiple_of(at - 16, 8), 8)
        for j in range(width // LANES):
            cols = slice(j * LANES, (j + 1) * LANES)
            updated_ref[to, cols] = base_ref[to, cols] + (
                d[0] * v0[j, here, :] + d[1] * v1[j, here, :] + d[2] * v2[j, here, :]
            )
        return c

    copies = []
    chunk = n // CHUNKS
    for k in range(CHUNKS):
        over_groups(1 + k * chunk // 8, 1 + (k + 1) * chunk // 8, emit, 0, 4)
        part = pl.ds(k * chunk, chunk)
        copies.append(pltpu.make_async_copy(updated_ref.at[part, :], updated_hbm.at[part, :], sems.at[k]))
        copies[-1].start()
    for copy in copies:
        copy.wait()


def params(mib):
    return pltpu.CompilerParams(vmem_limit_bytes=mib << 20)


VM = pl.BlockSpec(memory_space=pltpu.VMEM)
SM = pl.BlockSpec(memory_space=pltpu.SMEM)
HB = pl.BlockSpec(memory_space=pltpu.HBM)


def in_pairs(near, far, axis):
    size = lax.axis_size(axis)
    odd = [(i, ((i + 1) ^ 1) - 1) for i in range(1, size - 1)]
    got = lax.ppermute(far, axis, odd)
    return lax.ppermute(near, axis, [(i, i ^ 1) for i in range(size)]), got


def total(sums):
    size = sums.shape[0]
    sent = lax.all_to_all(sums.reshape(size, 1, LANES), ALL, 0, 0, tiled=True)
    return sent.reshape(size, LANES)


def body(phase, tile_mask):
    n, width = phase.shape
    f32 = jnp.float32
    sd = jax.ShapeDtypeStruct
    odd = jnp.stack([lax.axis_index(ROW) % 2, lax.axis_index(COL) % 2]).astype(jnp.int32)
    edge = sd((8, width + LANES), f32)
    near, far, own_mask = pl.pallas_call(
        strips_kernel,
        in_specs=[SM, HB, HB],
        out_specs=[VM] * 3,
        out_shape=[sd((8, n + LANES), f32)] * 2 + [sd((8, LANES), f32)],
        scratch_shapes=[
            pltpu.VMEM((n, LANES), f32),
            pltpu.VMEM((n, LANES), f32),
            pltpu.SMEM(tile_mask.shape, jnp.int32),
            pltpu.SemaphoreType.DMA((3,)),
        ],
        compiler_params=params(4),
        name="strips",
    )(odd, pltpu.with_memory_space_constraint(phase, pltpu.HBM), pltpu.with_memory_space_constraint(tile_mask, pltpu.HBM))
    near, far = in_pairs(near, far, COL)
    side, near, far, masks = pl.pallas_call(
        corners_kernel,
        in_specs=[SM] + [VM] * 4,
        out_specs=[VM] * 4,
        out_shape=[sd((n, LANES), f32), edge, edge, sd((2, 8, LANES), f32)],
        compiler_params=params(6),
        name="corners",
    )(odd, near, far, phase, own_mask)
    near, far = in_pairs(near, far, ROW)
    devices = 1
    for axis in ALL:
        devices *= lax.axis_size(axis)
    tiles = width // LANES + 1
    ext = sd((tiles, n + 32, LANES), f32)
    act = sd((tiles, 8 * (n // TILE + 2), LANES), f32)
    sums = sd((devices, LANES), f32)
    fields = [ext] * 5 + [act]
    *held, part = pl.pallas_call(
        inner_kernel,
        in_specs=[VM] * 4,
        out_specs=[VM] * 7,
        out_shape=fields + [sd((8, LANES), f32)],
        compiler_params=params(14),
        name="inner",
    )(phase, side, masks, own_mask)
    *held, part = pl.pallas_call(
        outer_kernel,
        in_specs=[SM] + [VM] * 9,
        out_specs=[VM] * 7,
        out_shape=fields + [sums],
        input_output_aliases={4 + i: i for i in range(6)},
        compiler_params=params(14),
        name="outer",
    )(odd, near, far, part, *held)
    p, w0, w1, w2, coef, act = held
    gathered = total(part)
    own = sd((n, width), f32)
    section, base, v0, v1, v2, part = pl.pallas_call(
        second_kernel,
        in_specs=[VM] * 7,
        out_specs=[HB] + [VM] * 5,
        out_shape=[own, own, ext, ext, ext, sums],
        scratch_shapes=[pltpu.VMEM((n, width), f32), pltpu.SemaphoreType.DMA(())],
        compiler_params=params(20),
        name="second",
    )(gathered, p, w0, w1, w2, coef, act)
    updated = pl.pallas_call(
        third_kernel,
        in_specs=[VM] * 5,
        out_specs=HB,
        out_shape=own,
        scratch_shapes=[pltpu.VMEM((n, width), f32), pltpu.SemaphoreType.DMA((CHUNKS,))],
        compiler_params=params(10),
        name="third",
    )(total(part), base, v0, v1, v2)
    return updated, section


def solution(mesh):
    split = Mesh(mesh.devices.reshape(4, 4, 4, 2), ALL)
    in_specs = (P(ROW, COL), P(ROW, COL))
    out_specs = (P(ROW, COL), P(ROW, COL))
    return jax.shard_map(body, mesh=split, in_specs=in_specs, out_specs=out_specs, check_vma=False)
```

time: 64.2 us -> 58.3 us (0.908)
  blocking collectives: 38.9 us -> 36.1 us
  local copies, waits for them, and re-layouts: 2.59 us -> 0.01 us
    all_to_all x2, blocking collectives: 38.9 us -> 36.1 us  [total(): sent = lax.all_to_all(sums.reshape(size, 1, LANES), ALL, 0, 0, tiled=True)]
    unnamed x10 -> x2, local copies, waits for them, and re-layouts: 2.59 us -> 0.01 us
    pallas_call x5 -> x6, Pallas kernels: 12.5 us -> 12.3 us  [the longest x1 4.05 us: body(): pl.pallas_call(second_kernel, in_specs=[VM] * 7, out_specs=[HB] + [VM] *...]
  transfers between devices with their start and end apart: 4 -> 4, of which waited for: 2 -> 1; matrix products, arithmetic and copies ran while one was open for 0% -> 0% of each run, Pallas kernels for 0% -> 6%
where the time goes in v3:
time: 58.3 us; the launch traced here: 58.1 us
  blocking collectives  36.1 us (62%)
  Pallas kernels  12.3 us (21%)
  starting transfers between devices  7.07 us (12%)
  waiting for transfers between devices  1.81 us (3%)
  between operations  0.72 us (1%)
    all_to_all x2, blocking collectives, total(): sent = lax.all_to_all(sums.reshape(size, 1, LANES), ALL, 0, 0, tiled=True)  36.1 us
    ppermute x2, starting transfers between devices, in_pairs(): got = lax.ppermute(far, axis, odd)  4.21 us
    pallas_call x1, Pallas kernels, body(): pl.pallas_call(second_kernel, in_specs=[VM] * 7, out_specs=[HB] + [VM] *...  4.05 us
    pallas_call x1, Pallas kernels, body(): pl.pallas_call(inner_kernel, in_specs=[VM] * 4, out_specs=[VM] * 7, out_s...  3.21 us
    ppermute x2, starting transfers between devices, in_pairs(): return (lax.ppermute(near, axis, [(i, i ^ 1) for i in range(size)]), got)  2.86 us
    pallas_call x1, Pallas kernels, body(): pl.pallas_call(strips_kernel, in_specs=[SM, HB, HB], out_specs=[VM] * 3,...  1.81 us
    ppermute x2, waiting for transfers between devices, in_pairs(): got = lax.ppermute(far, axis, odd)  1.81 us
    pallas_call x1, Pallas kernels, body(): pl.pallas_call(third_kernel, in_specs=[VM] * 5, out_specs=HB, out_shape=o...  1.5 us
  transfers between devices with their start and end apart: 4, of which 1 were waited for; matrix products, arithmetic and copies ran while one was open for 0% of the time, Pallas kernels for 6%

profile of v3, /device:TPU:1, one launch (start us, length us, event | category | flops | bytes accessed | tf_op | source)
XLA Modules:
  0.0 58.1 jit_solution(3599634934553375218)
XLA Ops:
  0.6 0.0 copy-start
  0.7 0.1 pad_add_fusion.odd_ref
  0.7 1.8 %strips.1 = (f32[8,640]{1,0:T(8,128)S(1)}, f32[8,640]{1,0:T(8,128)S(1)}, f32[8,128]{1,0:T(8,128)S(1)}) custom-call(s32[2]{0:T(128)S(1)} %pad_add_fusion.odd_ref, f32[512,512]{1,0:T(8,128)} %phase_ref.3, s32[2,2]{1,0:T(2,128)} %mask_hbm.1), custom_call_target="tpu_custom_call" | custom-call | tf_op jit(solution)/shard_map/strips/pallas_call | solution.py:477
  2.6 1.5 %collective-permute-start = (f32[8,640]{1,0:T(8,128)S(1)}, f32[8,640]{1,0:T(8,128)S(1)}, u32[]{:S(2)}, u32[]{:S(2)}) collective-permute-start(f32[8,640]{1,0:T(8,128)S(1)} %get-tuple-element.29), channel_id=1, source_target_pairs={{0,1},{1,0},{2,3},{3,2},{4,5},{5,4},{6,7},{7,6},{8,9},{9,8},{10,11... | collective-permute-start | bytes 61448 | tf_op jit(solution)/shard_map/ppermute | solution.py:462
  4.0 3.6 %collective-permute-start.1 = (f32[8,640]{1,0:T(8,128)S(1)}, f32[8,640]{1,0:T(8,128)S(1)}, u32[]{:S(2)}, u32[]{:S(2)}) collective-permute-start(f32[8,640]{1,0:T(8,128)S(1)} %get-tuple-element.30), channel_id=1, source_target_pairs={{1,2},{2,1},{3,4},{4,3},{5,6},{6,5},{9,10},{10,9},{11,12},{12,11},... | collective-permute-start | bytes 61448 | tf_op jit(solution)/shard_map/ppermute | solution.py:461
  7.6 0.0 collective-permute-done.near_in
  7.6 1.8 %collective-permute-done.1.far_in = f32[8,640]{1,0:T(8,128)S(1)} collective-permute-done((f32[8,640]{1,0:T(8,128)S(1)}, f32[8,640]{1,0:T(8,128)S(1)}, u32[]{:S(2)}, u32[]{:S(2)}) %collective-permute-start.1) | collective-permute-done | bytes 20512 | tf_op jit(solution)/shard_map/ppermute | solution.py:461
  9.4 0.0 copy-done
  9.4 0.7 %corners.1 = (f32[512,128]{1,0:T(8,128)S(1)}, f32[8,640]{1,0:T(8,128)S(1)}, f32[8,640]{1,0:T(8,128)S(1)}, f32[2,8,128]{2,1,0:T(8,128)S(1)}) custom-call(s32[2]{0:T(128)S(1)} %pad_add_fusion.odd_ref, f32[8,640]{1,0:T(8,128)S(1)} %collective-permute-done.near_in, f32[8,640]{1,0:T(8,128)S(1)} %collective-permute-done.1.far_in, f32[512,512]{1,0:T(8,128)S(1)} %copy-done, ...), custom_call_target="tpu_custom_call" | custom-call | tf_op jit(solution)/shard_map/corners/pallas_call | solution.py:492
  10.1 1.4 %collective-permute-start.2 = (f32[8,640]{1,0:T(8,128)S(1)}, f32[8,640]{1,0:T(8,128)S(1)}, u32[]{:S(2)}, u32[]{:S(2)}) collective-permute-start(f32[8,640]{1,0:T(8,128)S(1)} %get-tuple-element.32), channel_id=1, source_target_pairs={{0,8},{8,0},{16,24},{24,16},{32,40},{40,32},{48,56},{56,48},{64,72... | collective-permute-start | bytes 61448 | tf_op jit(solution)/shard_map/ppermute | solution.py:462
  11.5 0.7 %collective-permute-start.3 = (f32[8,640]{1,0:T(8,128)S(1)}, f32[8,640]{1,0:T(8,128)S(1)}, u32[]{:S(2)}, u32[]{:S(2)}) collective-permute-start(f32[8,640]{1,0:T(8,128)S(1)} %get-tuple-element.33), channel_id=1, source_target_pairs={{8,16},{16,8},{24,32},{32,24},{40,48},{48,40},{56,64},{64,56},{72,... | collective-permute-start | bytes 61448 | tf_op jit(solution)/shard_map/ppermute | solution.py:461
  12.2 3.2 %inner.1 = (f32[5,544,128]{2,1,0:T(8,128)S(1)}, f32[5,544,128]{2,1,0:T(8,128)S(1)}, f32[5,544,128]{2,1,0:T(8,128)S(1)}, f32[5,544,128]{2,1,0:T(8,128)S(1)}, f32[...) custom-call(f32[512,512]{1,0:T(8,128)S(1)} %copy-done, ...), custom_call_target="tpu_custom_call" | custom-call | tf_op jit(solution)/shard_map/inner/pallas_call | solution.py:509
  15.4 0.0 collective-permute-done.2.near_in
  15.4 0.0 collective-permute-done.3.far_in
  15.4 1.0 %outer.1 = (f32[5,544,128]{2,1,0:T(8,128)S(1)}, f32[5,544,128]{2,1,0:T(8,128)S(1)}, f32[5,544,128]{2,1,0:T(8,128)S(1)}, f32[5,544,128]{2,1,0:T(8,128)S(1)}, f32[...) custom-call(s32[2]{0:T(128)S(1)} %pad_add_fusion.odd_ref, ...), custom_call_target="tpu_custom_call", output_to_operand_aliasing={{0}: (4, {}), {1}: (5, {}), {2}: (6, {}), {3}: (7, {}), {4}... | custom-call | tf_op jit(solution)/shard_map/outer/pallas_call | solution.py:517
  16.4 22.2 %all_to_all.10 = f32[128,1,128]{2,1,0:T(1,128)S(1)} all-to-all(f32[128,1,128]{2,1,0:T(1,128)S(1)} %bitcast.12), channel_id=1, replica_groups=mesh['row_0'=4,'row_1'=4,'col_0'=4,'col_1'=2] {'row_0','row_1','col_0','..., dimensions={0} | all-to-all | bytes 131072 | tf_op jit(solution)/shard_map/all_to_all | solution.py:467
  38.7 4.0 %second.1 = (f32[512,512]{1,0:T(8,128)}, f32[512,512]{1,0:T(8,128)S(1)}, f32[5,544,128]{2,1,0:T(8,128)S(1)}, f32[5,544,128]{2,1,0:T(8,128)S(1)}, f32[5,544,128]{2,1,0:T(8,128)S(1)}, /*index=5*/f32[128,128]{1,0:T(8,128)S(1)}) custom-call(f32[128,128]{1,0:T(8,128)S(1)} %bitcast.10, f32[5,544,128]{2,1,0:T(8,128)S(1)} %get-tuple-element.44.p_ref, ...), custom_call_target="tpu_custom_call" | custom-call | tf_op jit(solution)/shard_map/second/pallas_call | solution.py:529
  42.7 13.8 %all_to_all.11 = f32[128,1,128]{2,1,0:T(1,128)S(1)} all-to-all(f32[128,1,128]{2,1,0:T(1,128)S(1)} %bitcast.13), channel_id=1, replica_groups=mesh['row_0'=4,'row_1'=4,'col_0'=4,'col_1'=2] {'row_0','row_1','col_0','..., dimensions={0} | all-to-all | bytes 131072 | tf_op jit(solution)/shard_map/all_to_all | solution.py:467
  56.6 1.5 %third.1 = f32[512,512]{1,0:T(8,128)} custom-call(f32[128,128]{1,0:T(8,128)S(1)} %bitcast.11, f32[512,512]{1,0:T(8,128)S(1)} %get-tuple-element.51.base_ref, f32[5,544,128]{2,1,0:T(8,128)S(1)} %get-tuple-element.52.v0, f32[5,544,128]{2,1,0:T(8,128)S(1)} %get-tuple-element.53.v1, f32[5,544,128]{2,1,0:T(8,128)S(1)} %get-tuple-element.54.v2), custom_call_target="tpu_custom_call" | custom-call | tf_op jit(solution)/shard_map/third/pallas_call | solution.py:538
Async XLA Ops:
  0.6 8.8 %copy-start = (f32[512,512]{1,0:T(8,128)S(1)}, f32[512,512]{1,0:T(8,128)}, u32[]{:S(2)}) copy-start(f32[512,512]{1,0:T(8,128)} %phase_ref.3) | copy-start | bytes 3145732
  2.6 5.0 %collective-permute-start = (f32[8,640]{1,0:T(8,128)S(1)}, f32[8,640]{1,0:T(8,128)S(1)}, u32[]{:S(2)}, u32[]{:S(2)}) collective-permute-start(f32[8,640]{1,0:T(8,128)S(1)} %get-tuple-element.29), channel_id=1, source_target_pairs={{0,1},{1,0},{2,3},{3,2},{4,5},{5,4},{6,7},{7,6},{8,9},{9,8},{10,11... | collective-permute-start | bytes 61448 | tf_op jit(solution)/shard_map/ppermute | solution.py:462
  4.0 5.4 %collective-permute-start.1 = (f32[8,640]{1,0:T(8,128)S(1)}, f32[8,640]{1,0:T(8,128)S(1)}, u32[]{:S(2)}, u32[]{:S(2)}) collective-permute-start(f32[8,640]{1,0:T(8,128)S(1)} %get-tuple-element.30), channel_id=1, source_target_pairs={{1,2},{2,1},{3,4},{4,3},{5,6},{6,5},{9,10},{10,9},{11,12},{12,11},... | collective-permute-start | bytes 61448 | tf_op jit(solution)/shard_map/ppermute | solution.py:461
  10.1 5.3 %collective-permute-start.2 = (f32[8,640]{1,0:T(8,128)S(1)}, f32[8,640]{1,0:T(8,128)S(1)}, u32[]{:S(2)}, u32[]{:S(2)}) collective-permute-start(f32[8,640]{1,0:T(8,128)S(1)} %get-tuple-element.32), channel_id=1, source_target_pairs={{0,8},{8,0},{16,24},{24,16},{32,40},{40,32},{48,56},{56,48},{64,72... | collective-permute-start | bytes 61448 | tf_op jit(solution)/shard_map/ppermute | solution.py:462
  11.5 3.9 %collective-permute-start.3 = (f32[8,640]{1,0:T(8,128)S(1)}, f32[8,640]{1,0:T(8,128)S(1)}, u32[]{:S(2)}, u32[]{:S(2)}) collective-permute-start(f32[8,640]{1,0:T(8,128)S(1)} %get-tuple-element.33), channel_id=1, source_target_pairs={{8,16},{16,8},{24,32},{32,24},{40,48},{48,40},{56,64},{64,56},{72,... | collective-permute-start | bytes 61448 | tf_op jit(solution)/shard_map/ppermute | solution.py:461

commit v4 on v3

--- a/solution.py
+++ b/solution.py
@@ -1,5 +1,3 @@
-import functools
-
 import jax
 import jax.numpy as jnp
 from jax import lax
@@ -8,11 +6,11 @@
 from jax.sharding import Mesh
 from jax.sharding import PartitionSpec as P
 
+
 TILE = 256
 ROW = ("row_0", "row_1")
 COL = ("col_0", "col_1")
 ALL = ROW + COL
-HALO = 8
 LANES = 128
 UNROLL = 33
 CHUNKS = 4
@@ -378,8 +376,10 @@
     tiles, rows, _ = p_ref.shape
     groups = (rows - 16) // 8
     r, hess = hessenberg(gathered_ref[...])
-    a = on_basis(r, phi_column(hess, 0.5, 1), 0.5)
-    f = on_basis(r, phi_column(hess, 1.0, 1), 1.0)
+    scale = jnp.where(lax.broadcasted_iota(jnp.int32, (8, LANES), 0) < 4, 0.5, 1.0)
+    coefs = on_basis(r, phi_column(hess, scale, 1), scale)
+    a = [jnp.broadcast_to(c[0:1], (8, LANES)) for c in coefs]
+    f = [jnp.broadcast_to(c[7:8], (8, LANES)) for c in coefs]
     blank = jnp.zeros((8, LANES), jnp.float32)
     for ref in (v0, v1, v2):
         for j in range(tiles):
@@ -395,7 +395,7 @@
             ws = [ref[j, here, :] for ref in (w0, w1, w2)]
             phase = p_ref[j, here, :]
             shift = a[0] * ws[0] + a[1] * ws[1] + a[2] * ws[2]
-            out = (-4.0 * acts[j]) * (shift * shift) * (shift + 3.0 * phase)
+            out = (acts[j] * (shift * shift)) * (shift + 3.0 * phase)
             v0[j, here, :] = out
             outs.append(out)
             if own and j < tiles - 1:
@@ -423,7 +423,7 @@
 def third_kernel(gathered_ref, base_ref, v0, v1, v2, updated_hbm, updated_ref, sems):
     n, width = base_ref.shape
     r, hess = hessenberg(gathered_ref[...])
-    d = on_basis(r, phi_column(hess, 1.0, 3), 32.0)
+    d = on_basis(r, phi_column(hess, 1.0, 3), -4.0 * 32.0)
 
     def emit(group, at, c):
         here = pl.ds(at, 8)
@@ -458,17 +458,18 @@
 def in_pairs(near, far, axis):
     size = lax.axis_size(axis)
     odd = [(i, ((i + 1) ^ 1) - 1) for i in range(1, size - 1)]
-    got = lax.ppermute(far, axis, odd)
-    return lax.ppermute(near, axis, [(i, i ^ 1) for i in range(size)]), got
+    far = lax.ppermute(far, axis, odd)
+    near = lax.ppermute(near, axis, [(i, i ^ 1) for i in range(size)])
+    return near, far
 
 
 def total(sums):
     size = sums.shape[0]
-    sent = lax.all_to_all(sums.reshape(size, 1, LANES), ALL, 0, 0, tiled=True)
+    sent = lax.all_to_all(sums.reshape(size, 1, LANES), ALL[::-1], 0, 0, tiled=True)
     return sent.reshape(size, LANES)
 
 
-def body(phase, tile_mask):
+def step(phase, tile_mask):
     n, width = phase.shape
     f32 = jnp.float32
     sd = jax.ShapeDtypeStruct
@@ -551,4 +552,4 @@
     split = Mesh(mesh.devices.reshape(4, 4, 4, 2), ALL)
     in_specs = (P(ROW, COL), P(ROW, COL))
     out_specs = (P(ROW, COL), P(ROW, COL))
-    return jax.shard_map(body, mesh=split, in_specs=in_specs, out_specs=out_specs, check_vma=False)
+    return jax.shard_map(step, mesh=split, in_specs=in_specs, out_specs=out_specs, check_vma=False)

time: 58.3 us -> 57.6 us (0.988)
  no operation moved by 1% of the time
where the time goes in v4:
time: 57.6 us; the launch traced here: 57.4 us
  blocking collectives  35.7 us (62%)
  Pallas kernels  12.1 us (21%)
  starting transfers between devices  7.07 us (12%)
  waiting for transfers between devices  1.81 us (3%)
  between operations  0.72 us (1%)
    all_to_all x2, blocking collectives, total(): lax.all_to_all(sums.reshape(size, 1, LANES), ALL[::-1], 0, 0, tiled=True)  35.7 us
    ppermute x2, starting transfers between devices, in_pairs(): far = lax.ppermute(far, axis, odd)  4.21 us
    pallas_call x1, Pallas kernels, step(): pl.pallas_call(second_kernel, in_specs=[VM] * 7, out_specs=[HB] + [VM] *...  3.81 us
    pallas_call x1, Pallas kernels, step(): pl.pallas_call(inner_kernel, in_specs=[VM] * 4, out_specs=[VM] * 7, out_s...  3.21 us
    ppermute x2, starting transfers between devices, in_pairs(): near = lax.ppermute(near, axis, [(i, i ^ 1) for i in range(size)])  2.86 us
    pallas_call x1, Pallas kernels, step(): pl.pallas_call(strips_kernel, in_specs=[SM, HB, HB], out_specs=[VM] * 3,...  1.81 us
    ppermute x2, waiting for transfers between devices, in_pairs(): far = lax.ppermute(far, axis, odd)  1.81 us
    pallas_call x1, Pallas kernels, step(): pl.pallas_call(third_kernel, in_specs=[VM] * 5, out_specs=HB, out_shape=o...  1.5 us
  transfers between devices with their start and end apart: 4, of which 1 were waited for; matrix products, arithmetic and copies ran while one was open for 0% of the time, Pallas kernels for 6%

profile of v4, /device:TPU:1, one launch (start us, length us, event | category | flops | bytes accessed | tf_op | source)
XLA Modules:
  0.0 57.4 jit_solution(3358622135847710894)
XLA Ops:
  0.6 0.0 copy-start
  0.7 0.1 pad_add_fusion.odd_ref
  0.7 1.8 %strips.1 = (f32[8,640]{1,0:T(8,128)S(1)}, f32[8,640]{1,0:T(8,128)S(1)}, f32[8,128]{1,0:T(8,128)S(1)}) custom-call(s32[2]{0:T(128)S(1)} %pad_add_fusion.odd_ref, f32[512,512]{1,0:T(8,128)} %phase_ref.3, s32[2,2]{1,0:T(2,128)} %mask_hbm.1), custom_call_target="tpu_custom_call" | custom-call | tf_op jit(solution)/shard_map/strips/pallas_call | solution.py:478
  2.6 1.5 %collective-permute-start = (f32[8,640]{1,0:T(8,128)S(1)}, f32[8,640]{1,0:T(8,128)S(1)}, u32[]{:S(2)}, u32[]{:S(2)}) collective-permute-start(f32[8,640]{1,0:T(8,128)S(1)} %get-tuple-element.29), channel_id=1, source_target_pairs={{0,1},{1,0},{2,3},{3,2},{4,5},{5,4},{6,7},{7,6},{8,9},{9,8},{10,11... | collective-permute-start | bytes 61448 | tf_op jit(solution)/shard_map/ppermute | solution.py:462
  4.0 3.6 %collective-permute-start.1 = (f32[8,640]{1,0:T(8,128)S(1)}, f32[8,640]{1,0:T(8,128)S(1)}, u32[]{:S(2)}, u32[]{:S(2)}) collective-permute-start(f32[8,640]{1,0:T(8,128)S(1)} %get-tuple-element.30), channel_id=1, source_target_pairs={{1,2},{2,1},{3,4},{4,3},{5,6},{6,5},{9,10},{10,9},{11,12},{12,11},... | collective-permute-start | bytes 61448 | tf_op jit(solution)/shard_map/ppermute | solution.py:461
  7.6 0.0 collective-permute-done.near_in
  7.6 1.8 %collective-permute-done.1.far_in = f32[8,640]{1,0:T(8,128)S(1)} collective-permute-done((f32[8,640]{1,0:T(8,128)S(1)}, f32[8,640]{1,0:T(8,128)S(1)}, u32[]{:S(2)}, u32[]{:S(2)}) %collective-permute-start.1) | collective-permute-done | bytes 20512 | tf_op jit(solution)/shard_map/ppermute | solution.py:461
  9.4 0.0 copy-done
  9.4 0.7 %corners.1 = (f32[512,128]{1,0:T(8,128)S(1)}, f32[8,640]{1,0:T(8,128)S(1)}, f32[8,640]{1,0:T(8,128)S(1)}, f32[2,8,128]{2,1,0:T(8,128)S(1)}) custom-call(s32[2]{0:T(128)S(1)} %pad_add_fusion.odd_ref, f32[8,640]{1,0:T(8,128)S(1)} %collective-permute-done.near_in, f32[8,640]{1,0:T(8,128)S(1)} %collective-permute-done.1.far_in, f32[512,512]{1,0:T(8,128)S(1)} %copy-done, ...), custom_call_target="tpu_custom_call" | custom-call | tf_op jit(solution)/shard_map/corners/pallas_call | solution.py:493
  10.1 1.4 %collective-permute-start.2 = (f32[8,640]{1,0:T(8,128)S(1)}, f32[8,640]{1,0:T(8,128)S(1)}, u32[]{:S(2)}, u32[]{:S(2)}) collective-permute-start(f32[8,640]{1,0:T(8,128)S(1)} %get-tuple-element.32), channel_id=1, source_target_pairs={{0,8},{8,0},{16,24},{24,16},{32,40},{40,32},{48,56},{56,48},{64,72... | collective-permute-start | bytes 61448 | tf_op jit(solution)/shard_map/ppermute | solution.py:462
  11.5 0.7 %collective-permute-start.3 = (f32[8,640]{1,0:T(8,128)S(1)}, f32[8,640]{1,0:T(8,128)S(1)}, u32[]{:S(2)}, u32[]{:S(2)}) collective-permute-start(f32[8,640]{1,0:T(8,128)S(1)} %get-tuple-element.33), channel_id=1, source_target_pairs={{8,16},{16,8},{24,32},{32,24},{40,48},{48,40},{56,64},{64,56},{72,... | collective-permute-start | bytes 61448 | tf_op jit(solution)/shard_map/ppermute | solution.py:461
  12.2 3.2 %inner.1 = (f32[5,544,128]{2,1,0:T(8,128)S(1)}, f32[5,544,128]{2,1,0:T(8,128)S(1)}, f32[5,544,128]{2,1,0:T(8,128)S(1)}, f32[5,544,128]{2,1,0:T(8,128)S(1)}, f32[...) custom-call(f32[512,512]{1,0:T(8,128)S(1)} %copy-done, ...), custom_call_target="tpu_custom_call" | custom-call | tf_op jit(solution)/shard_map/inner/pallas_call | solution.py:510
  15.4 0.0 collective-permute-done.2.near_in
  15.4 0.0 collective-permute-done.3.far_in
  15.4 1.0 %outer.1 = (f32[5,544,128]{2,1,0:T(8,128)S(1)}, f32[5,544,128]{2,1,0:T(8,128)S(1)}, f32[5,544,128]{2,1,0:T(8,128)S(1)}, f32[5,544,128]{2,1,0:T(8,128)S(1)}, f32[...) custom-call(s32[2]{0:T(128)S(1)} %pad_add_fusion.odd_ref, ...), custom_call_target="tpu_custom_call", output_to_operand_aliasing={{0}: (4, {}), {1}: (5, {}), {2}: (6, {}), {3}: (7, {}), {4}... | custom-call | tf_op jit(solution)/shard_map/outer/pallas_call | solution.py:518
  16.4 22.3 %all_to_all.10 = f32[128,1,128]{2,1,0:T(1,128)S(1)} all-to-all(f32[128,1,128]{2,1,0:T(1,128)S(1)} %bitcast.12), channel_id=1, replica_groups=mesh['row_0'=4,'row_1'=4,'col_0'=4,'col_1'=2] {'col_1','col_0','row_1','..., dimensions={0} | all-to-all | bytes 131072 | tf_op jit(solution)/shard_map/all_to_all | solution.py:468
  38.7 3.8 %second.1 = (f32[512,512]{1,0:T(8,128)}, f32[512,512]{1,0:T(8,128)S(1)}, f32[5,544,128]{2,1,0:T(8,128)S(1)}, f32[5,544,128]{2,1,0:T(8,128)S(1)}, f32[5,544,128]{2,1,0:T(8,128)S(1)}, /*index=5*/f32[128,128]{1,0:T(8,128)S(1)}) custom-call(f32[128,128]{1,0:T(8,128)S(1)} %bitcast.10, f32[5,544,128]{2,1,0:T(8,128)S(1)} %get-tuple-element.44.p_ref, ...), custom_call_target="tpu_custom_call" | custom-call | tf_op jit(solution)/shard_map/second/pallas_call | solution.py:530
  42.5 13.4 %all_to_all.11 = f32[128,1,128]{2,1,0:T(1,128)S(1)} all-to-all(f32[128,1,128]{2,1,0:T(1,128)S(1)} %bitcast.13), channel_id=1, replica_groups=mesh['row_0'=4,'row_1'=4,'col_0'=4,'col_1'=2] {'col_1','col_0','row_1','..., dimensions={0} | all-to-all | bytes 131072 | tf_op jit(solution)/shard_map/all_to_all | solution.py:468
  55.9 1.5 %third.1 = f32[512,512]{1,0:T(8,128)} custom-call(f32[128,128]{1,0:T(8,128)S(1)} %bitcast.11, f32[512,512]{1,0:T(8,128)S(1)} %get-tuple-element.51.base_ref, f32[5,544,128]{2,1,0:T(8,128)S(1)} %get-tuple-element.52.v0, f32[5,544,128]{2,1,0:T(8,128)S(1)} %get-tuple-element.53.v1, f32[5,544,128]{2,1,0:T(8,128)S(1)} %get-tuple-element.54.v2), custom_call_target="tpu_custom_call" | custom-call | tf_op jit(solution)/shard_map/third/pallas_call | solution.py:539
Async XLA Ops:
  0.6 8.8 %copy-start = (f32[512,512]{1,0:T(8,128)S(1)}, f32[512,512]{1,0:T(8,128)}, u32[]{:S(2)}) copy-start(f32[512,512]{1,0:T(8,128)} %phase_ref.3) | copy-start | bytes 3145732
  2.6 5.0 %collective-permute-start = (f32[8,640]{1,0:T(8,128)S(1)}, f32[8,640]{1,0:T(8,128)S(1)}, u32[]{:S(2)}, u32[]{:S(2)}) collective-permute-start(f32[8,640]{1,0:T(8,128)S(1)} %get-tuple-element.29), channel_id=1, source_target_pairs={{0,1},{1,0},{2,3},{3,2},{4,5},{5,4},{6,7},{7,6},{8,9},{9,8},{10,11... | collective-permute-start | bytes 61448 | tf_op jit(solution)/shard_map/ppermute | solution.py:462
  4.0 5.4 %collective-permute-start.1 = (f32[8,640]{1,0:T(8,128)S(1)}, f32[8,640]{1,0:T(8,128)S(1)}, u32[]{:S(2)}, u32[]{:S(2)}) collective-permute-start(f32[8,640]{1,0:T(8,128)S(1)} %get-tuple-element.30), channel_id=1, source_target_pairs={{1,2},{2,1},{3,4},{4,3},{5,6},{6,5},{9,10},{10,9},{11,12},{12,11},... | collective-permute-start | bytes 61448 | tf_op jit(solution)/shard_map/ppermute | solution.py:461
  10.1 5.3 %collective-permute-start.2 = (f32[8,640]{1,0:T(8,128)S(1)}, f32[8,640]{1,0:T(8,128)S(1)}, u32[]{:S(2)}, u32[]{:S(2)}) collective-permute-start(f32[8,640]{1,0:T(8,128)S(1)} %get-tuple-element.32), channel_id=1, source_target_pairs={{0,8},{8,0},{16,24},{24,16},{32,40},{40,32},{48,56},{56,48},{64,72... | collective-permute-start | bytes 61448 | tf_op jit(solution)/shard_map/ppermute | solution.py:462
  11.5 3.9 %collective-permute-start.3 = (f32[8,640]{1,0:T(8,128)S(1)}, f32[8,640]{1,0:T(8,128)S(1)}, u32[]{:S(2)}, u32[]{:S(2)}) collective-permute-start(f32[8,640]{1,0:T(8,128)S(1)} %get-tuple-element.33), channel_id=1, source_target_pairs={{8,16},{16,8},{24,32},{32,24},{40,48},{48,40},{56,64},{64,56},{72,... | collective-permute-start | bytes 61448 | tf_op jit(solution)/shard_map/ppermute | solution.py:461

commit v5 on v4

--- a/solution.py
+++ b/solution.py
@@ -1,3 +1,5 @@
+import functools
+
 import jax
 import jax.numpy as jnp
 from jax import lax
@@ -236,40 +238,51 @@
     return emit
 
 
-def strips_kernel(odd_ref, phase_hbm, mask_hbm, near_ref, far_ref, own_ref, left_ref, right_ref, mask_ref, sems):
+def rows_of(values):
+    sub = lax.broadcasted_iota(jnp.int32, (8, LANES), 0)
+    out = jnp.zeros((8, LANES), jnp.float32)
+    for k, v in enumerate(values):
+        out = jnp.where(sub == k, v, out)
+    return out
+
+
+def row_of(block, k):
+    return jnp.broadcast_to(block[k : k + 1], (8, LANES))
+
+
+def strips_kernel(odd_ref, phase_hbm, mask_hbm, near_ref, far_ref, own_ref, p_ref, mask_ref, sems):
     n, width = phase_hbm.shape
-    copies = [
-        pltpu.make_async_copy(phase_hbm.at[:, 0:LANES], left_ref, sems.at[0]),
-        pltpu.make_async_copy(phase_hbm.at[:, width - LANES : width], right_ref, sems.at[1]),
-        pltpu.make_async_copy(mask_hbm, mask_ref, sems.at[2]),
-    ]
-    for c in copies:
-        c.start()
-    for c in copies:
-        c.wait()
+    last = width // LANES - 1
+    copies = {}
+    for j in (0, last, *range(1, last)):
+        source = phase_hbm.at[:, j * LANES : (j + 1) * LANES]
+        copies[j] = pltpu.make_async_copy(source, p_ref.at[j, 16 : n + 16, :], sems.at[j])
+        copies[j].start()
+    mask_copy = pltpu.make_async_copy(mask_hbm, mask_ref, sems.at[last + 1])
+    mask_copy.start()
+    mask_copy.wait()
     odd = jnp.full((8, LANES), odd_ref[1], jnp.int32) > 0
     odd_n = jnp.full((8, n), odd_ref[1], jnp.int32) > 0
-    lane = lax.broadcasted_iota(jnp.int32, (8, LANES), 1)
+    tiles_r, tiles_c = mask_ref.shape
+    mask = [[mask_ref[t, c].astype(jnp.float32) for c in range(tiles_c)] for t in range(tiles_r)]
+    own_ref[...] = rows_of([v for row in mask for v in row])
+    copies[0].wait()
+    copies[last].wait()
     strips = []
-    for ref, rows, col in ((left_ref, 0, 0), (right_ref, LANES - 8, mask_ref.shape[1] - 1)):
-        extra = jnp.zeros((8, LANES), jnp.float32)
-        for t in range(mask_ref.shape[0]):
-            extra = extra + jnp.where(lane == t, mask_ref[t, col].astype(jnp.float32), 0.0)
-        strips.append((ref[...].T[rows : rows + 8, :], extra))
-    own = jnp.zeros((8, LANES), jnp.float32)
-    tiles_r, tiles_c = mask_ref.shape
-    for t in range(tiles_r):
-        for c in range(tiles_c):
-            own = jnp.where(lane == t * tiles_c + c, mask_ref[t, c].astype(jnp.float32), own)
-    own_ref[...] = own
+    for j, rows, col in ((0, 0, 0), (last, LANES - 8, -1)):
+        strip = p_ref[j, 16 : n + 16, :].T[rows : rows + 8, :]
+        strips.append((strip, rows_of([row[col] for row in mask])))
     left, right = strips
     for out, a, b in ((near_ref, left, right), (far_ref, right, left)):
         out[:, :n] = jnp.where(odd_n, a[0], b[0])
         out[:, n:] = jnp.where(odd, a[1], b[1])
-
-
-def corners_kernel(odd_ref, near_in, far_in, phase_ref, own_ref, side_ref, near_ref, far_ref, masks_ref):
-    n, width = phase_ref.shape
+    for j in range(1, last):
+        copies[j].wait()
+
+
+def corners_kernel(odd_ref, near_in, far_in, p_ref, own_ref, ends_ref, masks_ref, near_ref, far_ref):
+    tiles, rows, _ = p_ref.shape
+    n, width = rows - 32, LANES * (tiles - 1)
     tiles_r, tiles_c = n // TILE, width // TILE
     odd = jnp.full((8, LANES), odd_ref[1], jnp.int32) > 0
     odd_n = jnp.full((8, n), odd_ref[1], jnp.int32) > 0
@@ -277,26 +290,23 @@
     from_right = jnp.where(odd_n, far_in[:, :n], near_in[:, :n])
     mask_left = jnp.where(odd, near_in[:, n:], far_in[:, n:])
     mask_right = jnp.where(odd, far_in[:, n:], near_in[:, n:])
+    ends_ref[0] = from_right
+    ends_ref[1] = from_left
     masks_ref[0] = mask_left
     masks_ref[1] = mask_right
-    zeros = jnp.zeros((LANES - 16, n), jnp.float32)
-    side = jnp.concatenate([from_right, zeros, from_left], axis=0).T
-    side_ref[...] = side
-    lane = lax.broadcasted_iota(jnp.int32, (8, LANES), 1)
+    zeros = jnp.zeros((LANES - 16, LANES), jnp.float32)
+    own = own_ref[...]
+    odd_row = jnp.full((8, LANES), odd_ref[0], jnp.int32) > 0
     strips = []
-    for rows, t in ((0, 0), (n - 8, tiles_r - 1)):
-        extra = side[rows : rows + 8, :]
-        for c in range(tiles_c):
-            extra = jnp.where(lane == 16 + c, splat(own_ref[...], lane, t * tiles_c + c), extra)
-        extra = jnp.where(lane == 16 + tiles_c, splat(mask_right, lane, t), extra)
-        extra = jnp.where(lane == 17 + tiles_c, splat(mask_left, lane, t), extra)
-        strips.append((phase_ref[rows : rows + 8, :], extra))
+    for at, part, row, t in ((16, slice(0, LANES), 0, 0), (n + 8, slice(n - LANES, n), LANES - 8, tiles_r - 1)):
+        corner = jnp.concatenate([from_right[:, part], zeros, from_left[:, part]], axis=0).T[row : row + 8, :]
+        masks = [row_of(own, t * tiles_c + c) for c in range(tiles_c)]
+        masks += [row_of(mask_right, t), row_of(mask_left, t)]
+        strips.append([p_ref[j, at : at + 8, :] for j in range(tiles - 1)] + [corner, rows_of(masks)])
     up, down = strips
-    odd = jnp.full((8, LANES), odd_ref[0], jnp.int32) > 0
-    odd_w = jnp.full((8, width), odd_ref[0], jnp.int32) > 0
     for out, a, b in ((near_ref, up, down), (far_ref, down, up)):
-        out[:, :width] = jnp.where(odd_w, a[0], b[0])
-        out[:, width:] = jnp.where(odd, a[1], b[1])
+        for j in range(tiles + 1):
+            out[:, j * LANES : (j + 1) * LANES] = jnp.where(odd_row, a[j], b[j])
 
 
 def act_cells(act_ref, band, values, right, left):
@@ -317,18 +327,16 @@
     )
 
 
-def inner_kernel(phase_ref, side_in, masks_ref, own_ref, p_ref, w0, w1, w2, coef_ref, act_ref, sums_ref):
-    n, width = phase_ref.shape
-    tiles = p_ref.shape[0]
+def inner_kernel(ends_ref, masks_ref, own_ref, p_in, p_ref, w0, w1, w2, coef_ref, act_ref, sums_ref):
+    tiles, rows, _ = p_ref.shape
+    n, width = rows - 32, LANES * (tiles - 1)
     groups = n // 8 + 2
     tiles_r, tiles_c = n // TILE, width // TILE
-    lane = lax.broadcasted_iota(jnp.int32, (8, LANES), 1)
     for t in range(tiles_r):
-        values = [splat(own_ref[...], lane, t * tiles_c + c) for c in range(tiles_c)]
-        act_cells(act_ref, t + 1, values, splat(masks_ref[1], lane, t), splat(masks_ref[0], lane, t))
-    for j in range(tiles - 1):
-        p_ref[j, 16 : n + 16, :] = phase_ref[:, j * LANES : (j + 1) * LANES]
-    p_ref[tiles - 1, 16 : n + 16, :] = side_in[...]
+        values = [row_of(own_ref[...], t * tiles_c + c) for c in range(tiles_c)]
+        act_cells(act_ref, t + 1, values, row_of(masks_ref[1], t), row_of(masks_ref[0], t))
+    zeros = jnp.zeros((LANES - 16, n), jnp.float32)
+    p_ref[tiles - 1, 16 : n + 16, :] = jnp.concatenate([ends_ref[0], zeros, ends_ref[1]], axis=0).T
     sums = []
     for k, (emit, count) in enumerate(first_passes(p_ref, w0, w1, w2, coef_ref, act_ref)):
         sums += over_groups(2 + k, groups - 2 - k, emit, no_sums(count, tiles))
@@ -344,12 +352,13 @@
     groups = n // 8 + 2
     width = LANES * (tiles - 1)
     tiles_r, tiles_c = n // TILE, width // TILE
-    lane = lax.broadcasted_iota(jnp.int32, (8, LANES), 1)
     odd = jnp.full((8, LANES), odd_ref[0], jnp.int32) > 0
-    up = [jnp.where(odd, near_in[:, j * LANES : (j + 1) * LANES], far_in[:, j * LANES : (j + 1) * LANES]) for j in range(tiles)]
-    down = [jnp.where(odd, far_in[:, j * LANES : (j + 1) * LANES], near_in[:, j * LANES : (j + 1) * LANES]) for j in range(tiles)]
-    for t, extra in ((0, up[-1]), (tiles_r + 1, down[-1])):
-        values = [splat(extra, lane, 16 + c) for c in range(tiles_c + 2)]
+    near = [near_in[:, j * LANES : (j + 1) * LANES] for j in range(tiles + 1)]
+    far = [far_in[:, j * LANES : (j + 1) * LANES] for j in range(tiles + 1)]
+    *up, up_masks = [jnp.where(odd, a, b) for a, b in zip(near, far)]
+    *down, down_masks = [jnp.where(odd, b, a) for a, b in zip(near, far)]
+    for t, masks in ((0, up_masks), (tiles_r + 1, down_masks)):
+        values = [row_of(masks, c) for c in range(tiles_c + 2)]
         act_cells(act_ref, t, values[:tiles_c], values[tiles_c], values[tiles_c + 1])
     blank = jnp.zeros((8, LANES), jnp.float32)
     for ref in (p_ref, w0, w1, w2):
@@ -357,9 +366,8 @@
             ref[j, 0:8, :] = blank
             ref[j, n + 24 : n + 32, :] = blank
     for at, strip in ((8, up), (n + 16, down)):
-        for j in range(tiles - 1):
+        for j in range(tiles):
             p_ref[j, at : at + 8, :] = strip[j]
-        p_ref[tiles - 1, at : at + 8, :] = jnp.where((lane < 8) | (lane >= LANES - 8), strip[-1], 0.0)
     sums = []
     for k, (emit, count) in enumerate(first_passes(p_ref, w0, w1, w2, coef_ref, act_ref)):
         own = k == 3
@@ -399,7 +407,7 @@
             v0[j, here, :] = out
             outs.append(out)
             if own and j < tiles - 1:
-                to = pl.ds(pl.multiple_of(at - 16, 8), 8)
+                to = pl.ds(at - 16 if isinstance(at, int) else pl.multiple_of(at - 16, 8), 8)
                 cols = slice(j * LANES, (j + 1) * LANES)
                 section_ref[to, cols] = phase + shift
                 base_ref[to, cols] = phase + (f[0] * ws[0] + f[1] * ws[1] + f[2] * ws[2])
@@ -410,10 +418,18 @@
         part = over_groups(1, groups - 1, emit, part, most)
         return over_groups(groups - 1, groups, emit, part)
 
-    sums = [*sides(start, 1, 8)]
+    power = power_of(v0, v1, coef_ref, act_ref)
+
+    def fused(group, at, c):
+        return start(group, at, c[0]), power(group - 2, at - 16, c[1])
+
+    part = no_sums(1, tiles), no_sums(2, tiles)
+    part = over_groups(0, 3, start, part[0]), over_groups(0, 1, power, part[1])
+    part = over_groups(3, groups - 1, fused, part)
+    part = over_groups(groups - 1, groups, start, part[0]), part[1]
     copy = pltpu.make_async_copy(section_ref, section_hbm, sem)
     copy.start()
-    sums += sides(power_of(v0, v1, coef_ref, act_ref), 2, UNROLL)
+    sums = [*part[0], *over_groups(groups - 3, groups, power, part[1])]
     sums += sides(power_of(v1, v2, coef_ref, act_ref), 2, UNROLL)
     sums += over_groups(1, groups - 1, form_of(v2, coef_ref), no_sums(1, tiles))
     write_row(sum_row(sums), sums_ref)
@@ -474,37 +490,33 @@
     f32 = jnp.float32
     sd = jax.ShapeDtypeStruct
     odd = jnp.stack([lax.axis_index(ROW) % 2, lax.axis_index(COL) % 2]).astype(jnp.int32)
-    edge = sd((8, width + LANES), f32)
-    near, far, own_mask = pl.pallas_call(
+    tiles = width // LANES + 1
+    ext = sd((tiles, n + 32, LANES), f32)
+    act = sd((tiles, 8 * (n // TILE + 2), LANES), f32)
+    edge = sd((8, width + 2 * LANES), f32)
+    hbm = functools.partial(pltpu.with_memory_space_constraint, memory_space=pltpu.HBM)
+    near, far, own_mask, p = pl.pallas_call(
         strips_kernel,
         in_specs=[SM, HB, HB],
-        out_specs=[VM] * 3,
-        out_shape=[sd((8, n + LANES), f32)] * 2 + [sd((8, LANES), f32)],
-        scratch_shapes=[
-            pltpu.VMEM((n, LANES), f32),
-            pltpu.VMEM((n, LANES), f32),
-            pltpu.SMEM(tile_mask.shape, jnp.int32),
-            pltpu.SemaphoreType.DMA((3,)),
-        ],
-        compiler_params=params(4),
+        out_specs=[VM] * 4,
+        out_shape=[sd((8, n + LANES), f32)] * 2 + [sd((8, LANES), f32), ext],
+        scratch_shapes=[pltpu.SMEM(tile_mask.shape, jnp.int32), pltpu.SemaphoreType.DMA((tiles,))],
+        compiler_params=params(6),
         name="strips",
-    )(odd, pltpu.with_memory_space_constraint(phase, pltpu.HBM), pltpu.with_memory_space_constraint(tile_mask, pltpu.HBM))
+    )(odd, hbm(phase), hbm(tile_mask))
     near, far = in_pairs(near, far, COL)
-    side, near, far, masks = pl.pallas_call(
+    ends, masks, near, far = pl.pallas_call(
         corners_kernel,
         in_specs=[SM] + [VM] * 4,
         out_specs=[VM] * 4,
-        out_shape=[sd((n, LANES), f32), edge, edge, sd((2, 8, LANES), f32)],
+        out_shape=[sd((2, 8, n), f32), sd((2, 8, LANES), f32), edge, edge],
         compiler_params=params(6),
         name="corners",
-    )(odd, near, far, phase, own_mask)
+    )(odd, near, far, p, own_mask)
     near, far = in_pairs(near, far, ROW)
     devices = 1
     for axis in ALL:
         devices *= lax.axis_size(axis)
-    tiles = width // LANES + 1
-    ext = sd((tiles, n + 32, LANES), f32)
-    act = sd((tiles, 8 * (n // TILE + 2), LANES), f32)
     sums = sd((devices, LANES), f32)
     fields = [ext] * 5 + [act]
     *held, part = pl.pallas_call(
@@ -512,9 +524,10 @@
         in_specs=[VM] * 4,
         out_specs=[VM] * 7,
         out_shape=fields + [sd((8, LANES), f32)],
+        input_output_aliases={3: 0},
         compiler_params=params(14),
         name="inner",
-    )(phase, side, masks, own_mask)
+    )(ends, masks, own_mask, p)
     *held, part = pl.pallas_call(
         outer_kernel,
         in_specs=[SM] + [VM] * 9,

time: 57.6 us -> 57.3 us (level)
  no operation moved by 1% of the time
where the time goes in v5:
time: 57.3 us; the launch traced here: 57.1 us
  blocking collectives  35.7 us (62%)
  Pallas kernels  11.8 us (21%)
  starting transfers between devices  7.07 us (12%)
  waiting for transfers between devices  1.77 us (3%)
  between operations  0.71 us (1%)
    all_to_all x2, blocking collectives, total(): lax.all_to_all(sums.reshape(size, 1, LANES), ALL[::-1], 0, 0, tiled=True)  35.7 us
    ppermute x2, starting transfers between devices, in_pairs(): far = lax.ppermute(far, axis, odd)  4.21 us
    pallas_call x1, Pallas kernels, step(): pl.pallas_call(second_kernel, in_specs=[VM] * 7, out_specs=[HB] + [VM] *...  3.62 us
    pallas_call x1, Pallas kernels, step(): pl.pallas_call(inner_kernel, in_specs=[VM] * 4, out_specs=[VM] * 7, out_s...  3.27 us
    ppermute x2, starting transfers between devices, in_pairs(): near = lax.ppermute(near, axis, [(i, i ^ 1) for i in range(size)])  2.86 us
    pallas_call x1, Pallas kernels, step(): pl.pallas_call(strips_kernel, in_specs=[SM, HB, HB], out_specs=[VM] * 4,...  1.82 us
    ppermute x2, waiting for transfers between devices, in_pairs(): far = lax.ppermute(far, axis, odd)  1.76 us
    pallas_call x1, Pallas kernels, step(): pl.pallas_call(third_kernel, in_specs=[VM] * 5, out_specs=HB, out_shape=o...  1.5 us
  transfers between devices with their start and end apart: 4, of which 1 were waited for; matrix products, arithmetic and copies ran while one was open for 0% of the time, Pallas kernels for 6%

profile of v5, /device:TPU:1, one launch (start us, length us, event | category | flops | bytes accessed | tf_op | source)
XLA Modules:
  0.0 57.1 jit_solution(10684650429568844552)
XLA Ops:
  0.7 0.1 pad_add_fusion.odd_ref
  0.7 1.8 %strips.1 = (f32[8,640]{1,0:T(8,128)S(1)}, f32[8,640]{1,0:T(8,128)S(1)}, f32[8,128]{1,0:T(8,128)S(1)}, f32[5,544,128]{2,1,0:T(8,128)S(1)}) custom-call(s32[2]{0:T(128)S(1)} %pad_add_fusion.odd_ref, f32[512,512]{1,0:T(8,128)} %phase_hbm.1, s32[2,2]{1,0:T(2,128)} %mask_hbm.1), custom_call_target="tpu_custom_call" | custom-call | tf_op jit(solution)/shard_map/strips/pallas_call | solution.py:498
  2.6 1.5 %collective-permute-start = (f32[8,640]{1,0:T(8,128)S(1)}, f32[8,640]{1,0:T(8,128)S(1)}, u32[]{:S(2)}, u32[]{:S(2)}) collective-permute-start(f32[8,640]{1,0:T(8,128)S(1)} %get-tuple-element.30), channel_id=1, source_target_pairs={{0,1},{1,0},{2,3},{3,2},{4,5},{5,4},{6,7},{7,6},{8,9},{9,8},{10,11... | collective-permute-start | bytes 61448 | tf_op jit(solution)/shard_map/ppermute | solution.py:478
  4.0 3.6 %collective-permute-start.1 = (f32[8,640]{1,0:T(8,128)S(1)}, f32[8,640]{1,0:T(8,128)S(1)}, u32[]{:S(2)}, u32[]{:S(2)}) collective-permute-start(f32[8,640]{1,0:T(8,128)S(1)} %get-tuple-element.31), channel_id=1, source_target_pairs={{1,2},{2,1},{3,4},{4,3},{5,6},{6,5},{9,10},{10,9},{11,12},{12,11},... | collective-permute-start | bytes 61448 | tf_op jit(solution)/shard_map/ppermute | solution.py:477
  7.6 0.0 collective-permute-done.near_in
  7.6 1.8 %collective-permute-done.1.far_in = f32[8,640]{1,0:T(8,128)S(1)} collective-permute-done((f32[8,640]{1,0:T(8,128)S(1)}, f32[8,640]{1,0:T(8,128)S(1)}, u32[]{:S(2)}, u32[]{:S(2)}) %collective-permute-start.1) | collective-permute-done | bytes 20512 | tf_op jit(solution)/shard_map/ppermute | solution.py:477
  9.3 0.6 %corners.1 = (f32[2,8,512]{2,1,0:T(8,128)S(1)}, f32[2,8,128]{2,1,0:T(8,128)S(1)}, f32[8,768]{1,0:T(8,128)S(1)}, f32[8,768]{1,0:T(8,128)S(1)}) custom-call(s32[2]{0:T(128)S(1)} %pad_add_fusion.odd_ref, f32[8,640]{1,0:T(8,128)S(1)} %collective-permute-done.near_in, f32[8,640]{1,0:T(8,128)S(1)} %collective-permute-done.1.far_in, ...), custom_call_target="tpu_custom_call" | custom-call | tf_op jit(solution)/shard_map/corners/pallas_call | solution.py:508
  10.0 1.4 %collective-permute-start.2 = (f32[8,768]{1,0:T(8,128)S(1)}, f32[8,768]{1,0:T(8,128)S(1)}, u32[]{:S(2)}, u32[]{:S(2)}) collective-permute-start(f32[8,768]{1,0:T(8,128)S(1)} %get-tuple-element.34), channel_id=1, source_target_pairs={{0,8},{8,0},{16,24},{24,16},{32,40},{40,32},{48,56},{56,48},{64,72... | collective-permute-start | bytes 73736 | tf_op jit(solution)/shard_map/ppermute | solution.py:478
  11.4 0.7 %collective-permute-start.3 = (f32[8,768]{1,0:T(8,128)S(1)}, f32[8,768]{1,0:T(8,128)S(1)}, u32[]{:S(2)}, u32[]{:S(2)}) collective-permute-start(f32[8,768]{1,0:T(8,128)S(1)} %get-tuple-element.35), channel_id=1, source_target_pairs={{8,16},{16,8},{24,32},{32,24},{40,48},{48,40},{56,64},{64,56},{72,... | collective-permute-start | bytes 73736 | tf_op jit(solution)/shard_map/ppermute | solution.py:477
  12.0 3.3 %inner.1 = (f32[5,544,128]{2,1,0:T(8,128)S(1)}, f32[5,544,128]{2,1,0:T(8,128)S(1)}, f32[5,544,128]{2,1,0:T(8,128)S(1)}, f32[5,544,128]{2,1,0:T(8,128)S(1)}, f32[...) custom-call(f32[2,8,512]{2,1,0:T(8,128)S(1)} %get-tuple-element.36.e, ...), custom_call_target="tpu_custom_call", output_to_operand_aliasing={{0}: (3, {})} | custom-call | tf_op jit(solution)/shard_map/inner/pallas_call | solution.py:522
  15.3 0.0 collective-permute-done.2.near_in
  15.3 0.0 collective-permute-done.3.far_in
  15.3 1.0 %outer.1 = (f32[5,544,128]{2,1,0:T(8,128)S(1)}, f32[5,544,128]{2,1,0:T(8,128)S(1)}, f32[5,544,128]{2,1,0:T(8,128)S(1)}, f32[5,544,128]{2,1,0:T(8,128)S(1)}, f32[...) custom-call(s32[2]{0:T(128)S(1)} %pad_add_fusion.odd_ref, ...), custom_call_target="tpu_custom_call", output_to_operand_aliasing={{0}: (4, {}), {1}: (5, {}), {2}: (6, {}), {3}: (7, {}), {4}... | custom-call | tf_op jit(solution)/shard_map/outer/pallas_call | solution.py:531
  16.3 22.3 %all_to_all.10 = f32[128,1,128]{2,1,0:T(1,128)S(1)} all-to-all(f32[128,1,128]{2,1,0:T(1,128)S(1)} %bitcast.12), channel_id=1, replica_groups=mesh['row_0'=4,'row_1'=4,'col_0'=4,'col_1'=2] {'col_1','col_0','row_1','..., dimensions={0} | all-to-all | bytes 131072 | tf_op jit(solution)/shard_map/all_to_all | solution.py:484
  38.6 3.6 %second.1 = (f32[512,512]{1,0:T(8,128)}, f32[512,512]{1,0:T(8,128)S(1)}, f32[5,544,128]{2,1,0:T(8,128)S(1)}, f32[5,544,128]{2,1,0:T(8,128)S(1)}, f32[5,544,128]{2,1,0:T(8,128)S(1)}, /*index=5*/f32[128,128]{1,0:T(8,128)S(1)}) custom-call(f32[128,128]{1,0:T(8,128)S(1)} %bitcast.10, f32[5,544,128]{2,1,0:T(8,128)S(1)} %get-tuple-element.46.p_ref, ...), custom_call_target="tpu_custom_call" | custom-call | tf_op jit(solution)/shard_map/second/pallas_call | solution.py:543
  42.3 13.4 %all_to_all.11 = f32[128,1,128]{2,1,0:T(1,128)S(1)} all-to-all(f32[128,1,128]{2,1,0:T(1,128)S(1)} %bitcast.13), channel_id=1, replica_groups=mesh['row_0'=4,'row_1'=4,'col_0'=4,'col_1'=2] {'col_1','col_0','row_1','..., dimensions={0} | all-to-all | bytes 131072 | tf_op jit(solution)/shard_map/all_to_all | solution.py:484
  55.6 1.5 %third.1 = f32[512,512]{1,0:T(8,128)} custom-call(f32[128,128]{1,0:T(8,128)S(1)} %bitcast.11, f32[512,512]{1,0:T(8,128)S(1)} %get-tuple-element.53.base_ref, f32[5,544,128]{2,1,0:T(8,128)S(1)} %get-tuple-element.54.v0, f32[5,544,128]{2,1,0:T(8,128)S(1)} %get-tuple-element.55.v1, f32[5,544,128]{2,1,0:T(8,128)S(1)} %get-tuple-element.56.v2), custom_call_target="tpu_custom_call" | custom-call | tf_op jit(solution)/shard_map/third/pallas_call | solution.py:552
Async XLA Ops:
  2.6 5.0 %collective-permute-start = (f32[8,640]{1,0:T(8,128)S(1)}, f32[8,640]{1,0:T(8,128)S(1)}, u32[]{:S(2)}, u32[]{:S(2)}) collective-permute-start(f32[8,640]{1,0:T(8,128)S(1)} %get-tuple-element.30), channel_id=1, source_target_pairs={{0,1},{1,0},{2,3},{3,2},{4,5},{5,4},{6,7},{7,6},{8,9},{9,8},{10,11... | collective-permute-start | bytes 61448 | tf_op jit(solution)/shard_map/ppermute | solution.py:478
  4.0 5.3 %collective-permute-start.1 = (f32[8,640]{1,0:T(8,128)S(1)}, f32[8,640]{1,0:T(8,128)S(1)}, u32[]{:S(2)}, u32[]{:S(2)}) collective-permute-start(f32[8,640]{1,0:T(8,128)S(1)} %get-tuple-element.31), channel_id=1, source_target_pairs={{1,2},{2,1},{3,4},{4,3},{5,6},{6,5},{9,10},{10,9},{11,12},{12,11},... | collective-permute-start | bytes 61448 | tf_op jit(solution)/shard_map/ppermute | solution.py:477
  10.0 5.3 %collective-permute-start.2 = (f32[8,768]{1,0:T(8,128)S(1)}, f32[8,768]{1,0:T(8,128)S(1)}, u32[]{:S(2)}, u32[]{:S(2)}) collective-permute-start(f32[8,768]{1,0:T(8,128)S(1)} %get-tuple-element.34), channel_id=1, source_target_pairs={{0,8},{8,0},{16,24},{24,16},{32,40},{40,32},{48,56},{56,48},{64,72... | collective-permute-start | bytes 73736 | tf_op jit(solution)/shard_map/ppermute | solution.py:478
  11.4 3.9 %collective-permute-start.3 = (f32[8,768]{1,0:T(8,128)S(1)}, f32[8,768]{1,0:T(8,128)S(1)}, u32[]{:S(2)}, u32[]{:S(2)}) collective-permute-start(f32[8,768]{1,0:T(8,128)S(1)} %get-tuple-element.35), channel_id=1, source_target_pairs={{8,16},{16,8},{24,32},{32,24},{40,48},{48,40},{56,64},{64,56},{72,... | collective-permute-start | bytes 73736 | tf_op jit(solution)/shard_map/ppermute | solution.py:477

commit v6 on v5

--- a/solution.py
+++ b/solution.py
@@ -120,8 +120,8 @@
     sub = lax.broadcasted_iota(jnp.int32, (8, LANES), 0)
     lane = lax.broadcasted_iota(jnp.int32, (8, LANES), 1)
     rows = jnp.zeros((8, LANES), jnp.float32)
-    for n, tiles in enumerate(sums):
-        part = jnp.sum(sum(tiles[1:], tiles[0]), axis=0, keepdims=True)
+    for n, s in enumerate(sums):
+        part = jnp.sum(s, axis=0, keepdims=True)
         rows = jnp.where(sub == n, part, rows)
     values = jnp.sum(rows, axis=1, keepdims=True)
     row = jnp.sum(jnp.where(lane == sub, values, 0.0), axis=0, keepdims=True)
@@ -169,14 +169,18 @@
     return not isinstance(group, int) or 0 < group < groups - 1
 
 
-def add_products(sums, pairs):
-    return tuple(
-        tuple(s + a[j] * b[j] for j, s in enumerate(row)) for row, (a, b) in zip(sums, pairs)
-    )
-
-
-def no_sums(count, tiles):
-    return tuple(tuple(jnp.zeros((8, LANES), jnp.float32) for _ in range(tiles - 1)) for _ in range(count))
+def add_products(sums, pairs, own):
+    out = []
+    for s, (a, b) in zip(sums, pairs):
+        terms = [x * y for x, y in zip(a[:own], b[:own])]
+        while len(terms) > 1:
+            terms = [x + y for x, y in zip(terms[::2], terms[1::2])] + terms[len(terms) & ~1 :]
+        out.append(s + terms[0])
+    return tuple(out)
+
+
+def no_sums(count):
+    return tuple(jnp.zeros((8, LANES), jnp.float32) for _ in range(count))
 
 
 def power_of(src, dst, coef_ref, act_ref):
@@ -195,7 +199,7 @@
             dst[j, here, :] = out
             mids.append(mid)
             outs.append(out)
-        return add_products(sums, ((mids, outs), (outs, outs))) if is_own(group, groups) else sums
+        return add_products(sums, ((mids, outs), (outs, outs)), tiles - 1) if is_own(group, groups) else sums
 
     return emit
 
@@ -211,7 +215,7 @@
             mid = src[j, here, :]
             images.append(0.5 * (side[j] + src[j, pl.ds(at - 1, 8), :]) + coef_ref[j, here, :] * mid)
             mids.append(mid)
-        return add_products(sums, ((mids, images),))
+        return add_products(sums, ((mids, images),), tiles - 1)
 
     return emit
 
@@ -233,7 +237,7 @@
             w0[j, here, :] = out
             coef_ref[j, here, :] = acts[j] * (0.5 - 1.5 * square)
             outs.append(out)
-        return add_products(sums, ((outs, outs),)) if is_own(group, groups) else sums
+        return add_products(sums, ((outs, outs),), tiles - 1) if is_own(group, groups) else sums
 
     return emit
 
@@ -339,7 +343,7 @@
     p_ref[tiles - 1, 16 : n + 16, :] = jnp.concatenate([ends_ref[0], zeros, ends_ref[1]], axis=0).T
     sums = []
     for k, (emit, count) in enumerate(first_passes(p_ref, w0, w1, w2, coef_ref, act_ref)):
-        sums += over_groups(2 + k, groups - 2 - k, emit, no_sums(count, tiles))
+        sums += over_groups(2 + k, groups - 2 - k, emit, no_sums(count))
     sums_ref[...] = sum_row(sums)
 
 
@@ -371,7 +375,7 @@
     sums = []
     for k, (emit, count) in enumerate(first_passes(p_ref, w0, w1, w2, coef_ref, act_ref)):
         own = k == 3
-        part = no_sums(count, tiles)
+        part = no_sums(count)
         part = over_groups(1 if own else 0, 2 + k, emit, part)
         sums += over_groups(groups - 2 - k, groups - 1 if own else groups, emit, part)
     write_row(sum_row(sums) + inner_ref[...], sums_ref)
@@ -411,10 +415,10 @@
                 cols = slice(j * LANES, (j + 1) * LANES)
                 section_ref[to, cols] = phase + shift
                 base_ref[to, cols] = phase + (f[0] * ws[0] + f[1] * ws[1] + f[2] * ws[2])
-        return add_products(sums, ((outs, outs),)) if own else sums
+        return add_products(sums, ((outs, outs),), tiles - 1) if own else sums
 
     def sides(emit, count, most):
-        part = over_groups(0, 1, emit, no_sums(count, tiles))
+        part = over_groups(0, 1, emit, no_sums(count))
         part = over_groups(1, groups - 1, emit, part, most)
         return over_groups(groups - 1, groups, emit, part)
 
@@ -423,7 +427,7 @@
     def fused(group, at, c):
         return start(group, at, c[0]), power(group - 2, at - 16, c[1])
 
-    part = no_sums(1, tiles), no_sums(2, tiles)
+    part = no_sums(1), no_sums(2)
     part = over_groups(0, 3, start, part[0]), over_groups(0, 1, power, part[1])
     part = over_groups(3, groups - 1, fused, part)
     part = over_groups(groups - 1, groups, start, part[0]), part[1]
@@ -431,7 +435,7 @@
     copy.start()
     sums = [*part[0], *over_groups(groups - 3, groups, power, part[1])]
     sums += sides(power_of(v1, v2, coef_ref, act_ref), 2, UNROLL)
-    sums += over_groups(1, groups - 1, form_of(v2, coef_ref), no_sums(1, tiles))
+    sums += over_groups(1, groups - 1, form_of(v2, coef_ref), no_sums(1))
     write_row(sum_row(sums), sums_ref)
     copy.wait()
 

time: 57.3 us -> 57.3 us (level)
  no operation moved by 1% of the time
where the time goes in v6:
time: 57.3 us; the launch traced here: 57.1 us
  blocking collectives  35.7 us (62%)
  Pallas kernels  11.8 us (21%)
  starting transfers between devices  7.07 us (12%)
  waiting for transfers between devices  1.77 us (3%)
  between operations  0.71 us (1%)
    all_to_all x2, blocking collectives, total(): lax.all_to_all(sums.reshape(size, 1, LANES), ALL[::-1], 0, 0, tiled=True)  35.7 us
    ppermute x2, starting transfers between devices, in_pairs(): far = lax.ppermute(far, axis, odd)  4.21 us
    pallas_call x1, Pallas kernels, step(): pl.pallas_call(second_kernel, in_specs=[VM] * 7, out_specs=[HB] + [VM] *...  3.57 us
    pallas_call x1, Pallas kernels, step(): pl.pallas_call(inner_kernel, in_specs=[VM] * 4, out_specs=[VM] * 7, out_s...  3.27 us
    ppermute x2, starting transfers between devices, in_pairs(): near = lax.ppermute(near, axis, [(i, i ^ 1) for i in range(size)])  2.86 us
    pallas_call x1, Pallas kernels, step(): pl.pallas_call(strips_kernel, in_specs=[SM, HB, HB], out_specs=[VM] * 4,...  1.82 us
    ppermute x2, waiting for transfers between devices, in_pairs(): far = lax.ppermute(far, axis, odd)  1.76 us
    pallas_call x1, Pallas kernels, step(): pl.pallas_call(third_kernel, in_specs=[VM] * 5, out_specs=HB, out_shape=o...  1.5 us
  transfers between devices with their start and end apart: 4, of which 1 were waited for; matrix products, arithmetic and copies ran while one was open for 0% of the time, Pallas kernels for 6%

profile of v6, /device:TPU:1, one launch (start us, length us, event | category | flops | bytes accessed | tf_op | source)
XLA Modules:
  0.0 57.1 jit_solution(13233691499382501942)
XLA Ops:
  0.7 0.1 pad_add_fusion.odd_ref
  0.7 1.8 %strips.1 = (f32[8,640]{1,0:T(8,128)S(1)}, f32[8,640]{1,0:T(8,128)S(1)}, f32[8,128]{1,0:T(8,128)S(1)}, f32[5,544,128]{2,1,0:T(8,128)S(1)}) custom-call(s32[2]{0:T(128)S(1)} %pad_add_fusion.odd_ref, f32[512,512]{1,0:T(8,128)} %phase_hbm.1, s32[2,2]{1,0:T(2,128)} %mask_hbm.1), custom_call_target="tpu_custom_call" | custom-call | tf_op jit(solution)/shard_map/strips/pallas_call | solution.py:502
  2.6 1.5 %collective-permute-start = (f32[8,640]{1,0:T(8,128)S(1)}, f32[8,640]{1,0:T(8,128)S(1)}, u32[]{:S(2)}, u32[]{:S(2)}) collective-permute-start(f32[8,640]{1,0:T(8,128)S(1)} %get-tuple-element.30), channel_id=1, source_target_pairs={{0,1},{1,0},{2,3},{3,2},{4,5},{5,4},{6,7},{7,6},{8,9},{9,8},{10,11... | collective-permute-start | bytes 61448 | tf_op jit(solution)/shard_map/ppermute | solution.py:482
  4.0 3.6 %collective-permute-start.1 = (f32[8,640]{1,0:T(8,128)S(1)}, f32[8,640]{1,0:T(8,128)S(1)}, u32[]{:S(2)}, u32[]{:S(2)}) collective-permute-start(f32[8,640]{1,0:T(8,128)S(1)} %get-tuple-element.31), channel_id=1, source_target_pairs={{1,2},{2,1},{3,4},{4,3},{5,6},{6,5},{9,10},{10,9},{11,12},{12,11},... | collective-permute-start | bytes 61448 | tf_op jit(solution)/shard_map/ppermute | solution.py:481
  7.6 0.0 collective-permute-done.near_in
  7.6 1.8 %collective-permute-done.1.far_in = f32[8,640]{1,0:T(8,128)S(1)} collective-permute-done((f32[8,640]{1,0:T(8,128)S(1)}, f32[8,640]{1,0:T(8,128)S(1)}, u32[]{:S(2)}, u32[]{:S(2)}) %collective-permute-start.1) | collective-permute-done | bytes 20512 | tf_op jit(solution)/shard_map/ppermute | solution.py:481
  9.3 0.6 %corners.1 = (f32[2,8,512]{2,1,0:T(8,128)S(1)}, f32[2,8,128]{2,1,0:T(8,128)S(1)}, f32[8,768]{1,0:T(8,128)S(1)}, f32[8,768]{1,0:T(8,128)S(1)}) custom-call(s32[2]{0:T(128)S(1)} %pad_add_fusion.odd_ref, f32[8,640]{1,0:T(8,128)S(1)} %collective-permute-done.near_in, f32[8,640]{1,0:T(8,128)S(1)} %collective-permute-done.1.far_in, ...), custom_call_target="tpu_custom_call" | custom-call | tf_op jit(solution)/shard_map/corners/pallas_call | solution.py:512
  10.0 1.4 %collective-permute-start.2 = (f32[8,768]{1,0:T(8,128)S(1)}, f32[8,768]{1,0:T(8,128)S(1)}, u32[]{:S(2)}, u32[]{:S(2)}) collective-permute-start(f32[8,768]{1,0:T(8,128)S(1)} %get-tuple-element.34), channel_id=1, source_target_pairs={{0,8},{8,0},{16,24},{24,16},{32,40},{40,32},{48,56},{56,48},{64,72... | collective-permute-start | bytes 73736 | tf_op jit(solution)/shard_map/ppermute | solution.py:482
  11.4 0.7 %collective-permute-start.3 = (f32[8,768]{1,0:T(8,128)S(1)}, f32[8,768]{1,0:T(8,128)S(1)}, u32[]{:S(2)}, u32[]{:S(2)}) collective-permute-start(f32[8,768]{1,0:T(8,128)S(1)} %get-tuple-element.35), channel_id=1, source_target_pairs={{8,16},{16,8},{24,32},{32,24},{40,48},{48,40},{56,64},{64,56},{72,... | collective-permute-start | bytes 73736 | tf_op jit(solution)/shard_map/ppermute | solution.py:481
  12.0 3.3 %inner.1 = (f32[5,544,128]{2,1,0:T(8,128)S(1)}, f32[5,544,128]{2,1,0:T(8,128)S(1)}, f32[5,544,128]{2,1,0:T(8,128)S(1)}, f32[5,544,128]{2,1,0:T(8,128)S(1)}, f32[...) custom-call(f32[2,8,512]{2,1,0:T(8,128)S(1)} %get-tuple-element.36.e, ...), custom_call_target="tpu_custom_call", output_to_operand_aliasing={{0}: (3, {})} | custom-call | tf_op jit(solution)/shard_map/inner/pallas_call | solution.py:526
  15.3 0.0 collective-permute-done.2.near_in
  15.3 0.0 collective-permute-done.3.far_in
  15.3 1.0 %outer.1 = (f32[5,544,128]{2,1,0:T(8,128)S(1)}, f32[5,544,128]{2,1,0:T(8,128)S(1)}, f32[5,544,128]{2,1,0:T(8,128)S(1)}, f32[5,544,128]{2,1,0:T(8,128)S(1)}, f32[...) custom-call(s32[2]{0:T(128)S(1)} %pad_add_fusion.odd_ref, ...), custom_call_target="tpu_custom_call", output_to_operand_aliasing={{0}: (4, {}), {1}: (5, {}), {2}: (6, {}), {3}: (7, {}), {4}... | custom-call | tf_op jit(solution)/shard_map/outer/pallas_call | solution.py:535
  16.3 22.3 %all_to_all.10 = f32[128,1,128]{2,1,0:T(1,128)S(1)} all-to-all(f32[128,1,128]{2,1,0:T(1,128)S(1)} %bitcast.12), channel_id=1, replica_groups=mesh['row_0'=4,'row_1'=4,'col_0'=4,'col_1'=2] {'col_1','col_0','row_1','..., dimensions={0} | all-to-all | bytes 131072 | tf_op jit(solution)/shard_map/all_to_all | solution.py:488
  38.6 3.6 %second.1 = (f32[512,512]{1,0:T(8,128)}, f32[512,512]{1,0:T(8,128)S(1)}, f32[5,544,128]{2,1,0:T(8,128)S(1)}, f32[5,544,128]{2,1,0:T(8,128)S(1)}, f32[5,544,128]{2,1,0:T(8,128)S(1)}, /*index=5*/f32[128,128]{1,0:T(8,128)S(1)}) custom-call(f32[128,128]{1,0:T(8,128)S(1)} %bitcast.10, f32[5,544,128]{2,1,0:T(8,128)S(1)} %get-tuple-element.46.p_ref, ...), custom_call_target="tpu_custom_call" | custom-call | tf_op jit(solution)/shard_map/second/pallas_call | solution.py:547
  42.2 13.4 %all_to_all.11 = f32[128,1,128]{2,1,0:T(1,128)S(1)} all-to-all(f32[128,1,128]{2,1,0:T(1,128)S(1)} %bitcast.13), channel_id=1, replica_groups=mesh['row_0'=4,'row_1'=4,'col_0'=4,'col_1'=2] {'col_1','col_0','row_1','..., dimensions={0} | all-to-all | bytes 131072 | tf_op jit(solution)/shard_map/all_to_all | solution.py:488
  55.6 1.5 %third.1 = f32[512,512]{1,0:T(8,128)} custom-call(f32[128,128]{1,0:T(8,128)S(1)} %bitcast.11, f32[512,512]{1,0:T(8,128)S(1)} %get-tuple-element.53.base_ref, f32[5,544,128]{2,1,0:T(8,128)S(1)} %get-tuple-element.54.v0, f32[5,544,128]{2,1,0:T(8,128)S(1)} %get-tuple-element.55.v1, f32[5,544,128]{2,1,0:T(8,128)S(1)} %get-tuple-element.56.v2), custom_call_target="tpu_custom_call" | custom-call | tf_op jit(solution)/shard_map/third/pallas_call | solution.py:556
Async XLA Ops:
  2.6 5.0 %collective-permute-start = (f32[8,640]{1,0:T(8,128)S(1)}, f32[8,640]{1,0:T(8,128)S(1)}, u32[]{:S(2)}, u32[]{:S(2)}) collective-permute-start(f32[8,640]{1,0:T(8,128)S(1)} %get-tuple-element.30), channel_id=1, source_target_pairs={{0,1},{1,0},{2,3},{3,2},{4,5},{5,4},{6,7},{7,6},{8,9},{9,8},{10,11... | collective-permute-start | bytes 61448 | tf_op jit(solution)/shard_map/ppermute | solution.py:482
  4.0 5.3 %collective-permute-start.1 = (f32[8,640]{1,0:T(8,128)S(1)}, f32[8,640]{1,0:T(8,128)S(1)}, u32[]{:S(2)}, u32[]{:S(2)}) collective-permute-start(f32[8,640]{1,0:T(8,128)S(1)} %get-tuple-element.31), channel_id=1, source_target_pairs={{1,2},{2,1},{3,4},{4,3},{5,6},{6,5},{9,10},{10,9},{11,12},{12,11},... | collective-permute-start | bytes 61448 | tf_op jit(solution)/shard_map/ppermute | solution.py:481
  10.0 5.3 %collective-permute-start.2 = (f32[8,768]{1,0:T(8,128)S(1)}, f32[8,768]{1,0:T(8,128)S(1)}, u32[]{:S(2)}, u32[]{:S(2)}) collective-permute-start(f32[8,768]{1,0:T(8,128)S(1)} %get-tuple-element.34), channel_id=1, source_target_pairs={{0,8},{8,0},{16,24},{24,16},{32,40},{40,32},{48,56},{56,48},{64,72... | collective-permute-start | bytes 73736 | tf_op jit(solution)/shard_map/ppermute | solution.py:482
  11.4 3.9 %collective-permute-start.3 = (f32[8,768]{1,0:T(8,128)S(1)}, f32[8,768]{1,0:T(8,128)S(1)}, u32[]{:S(2)}, u32[]{:S(2)}) collective-permute-start(f32[8,768]{1,0:T(8,128)S(1)} %get-tuple-element.35), channel_id=1, source_target_pairs={{8,16},{16,8},{24,32},{32,24},{40,48},{48,40},{56,64},{64,56},{72,... | collective-permute-start | bytes 73736 | tf_op jit(solution)/shard_map/ppermute | solution.py:481
